TPU v7x, 32 devices: a whole 2x2x4 slice. The times are simulated.
32 devices in a mesh: dom: 32 (over z, y, x, core).
Axes of the slice: x: 2, y: 2, z: 4, core: 2. Of those that a mesh axis runs over, the one named last changes fastest.
Arguments:
- features: bfloat16 [524288, 256], P('dom'), may hold values from -48 to 48, as said below
- w_first: bfloat16 [1280, 256], replicated, may hold values from -0.15625 to 0.15625
- w_second: bfloat16 [1280, 256], replicated, may hold values from -0.15625 to 0.15625
- seed_owner: int32 [9216, 1], P('dom'), may hold values from 0 to 31; in each aligned block of 288 rows (0 to 287, 288 to 575, ...) at most 18 rows name the same one
- seed_row: int32 [9216], P('dom'), may hold values from 0 to 16383
- hop1_owner: int32 [36864, 1], P('dom'), may hold values from 0 to 31; in each aligned block of 1152 rows (0 to 1151, 1152 to 2303, ...) at most 72 rows name the same one
- hop1_row: int32 [36864], P('dom'), may hold values from 0 to 16383
- hop1_rel: int32 [36864], P('dom'), may hold values from 0 to 3
- hop2_owner: int32 [73728, 1], P('dom'), may hold values from 0 to 31; in each aligned block of 2304 rows (0 to 2303, 2304 to 4607, ...) at most 144 rows name the same one
- hop2_row: int32 [73728], P('dom'), may hold values from 0 to 16383
- hop2_rel: int32 [73728], P('dom'), may hold values from 0 to 3
- edge_mask: int32 [4096], P('dom'), may hold values 0 or 1
Outputs:
- edge_loss: float32 [4096], P('dom')
- mean_loss: float32 [], replicated
Inputs may be any that keep to these rules, and one draw needn't show every extreme that they name: `features`: standard normal entries; in some draws each row is scaled by a factor up to 10. `seed_owner`: among the rows of one device no owner is named by more than 18 rows; some owner is named by exactly 18 in every draw. `hop1_owner`: among the rows of one device no owner is named by more than 72 rows; some owner is named by exactly 72 in every draw. `hop2_owner`: among the rows of one device no owner is named by more than 144 rows; some owner is named by exactly 144 in every draw.
All inputs are finite; a program needn't handle non-finite values. No bound on the sum of `edge_mask` on one device may be relied on, other than what follows from the above.
Results may differ from a plain program's by a relative error of at most 0.002.
Values may be sent and summed in bfloat16 or wider, within the bound.
A program may use at most 64 MiB of HBM per device.

v0:
```python
import functools

import jax
import jax.numpy as jnp
import numpy as np
from jax import lax
from jax.experimental import pallas as pl
from jax.experimental.pallas import tpu as pltpu
from jax.sharding import PartitionSpec as P

MESH = pl.DeviceIdType.MESH
HOP = 11
PIECE = 96
LANES = 128
LOADS = 8

R = 4
BLOCK = 128
NEG = 32
FAN1 = 4
FAN2 = 2


def round_up(value, multiple):
    return (value + multiple - 1) // multiple * multiple


def unroll_of(count):
    return max(step for step in range(1, 25) if count % step == 0)


def bucket_all(owners, rows, group, sets, caps, bases, strides, devices):
    blocks = owners.shape[0] // group
    onehot = owners[:, None] == jnp.arange(devices, dtype=jnp.int32)[None, :]
    hot = onehot.astype(jnp.bfloat16).reshape(blocks, group, devices)
    counter = jnp.arange(group, dtype=jnp.int32)
    earlier = (counter[:, None] > counter[None, :]).astype(jnp.bfloat16)
    prior = jnp.einsum("ij,bjd->bid", earlier, hot, preferred_element_type=jnp.float32)
    totals = jnp.sum(hot.astype(jnp.float32), axis=1)
    carry = []
    start = 0
    for count in sets:
        running = jnp.zeros((devices,), jnp.float32)
        for block in range(start, start + count):
            carry.append(running)
            running = running + totals[block]
        start += count
    prior = prior + jnp.stack(carry)[:, None, :]
    position = jnp.sum(prior * hot.astype(jnp.float32), axis=2).astype(jnp.int32)
    offsets = np.concatenate([[0], np.cumsum(caps)[:-1]])
    offset = jnp.asarray(np.repeat(offsets, sets), jnp.int32)
    base = jnp.asarray(np.repeat(np.asarray(bases), sets), jnp.int32)
    stride = jnp.asarray(np.repeat(np.asarray(strides), sets), jnp.int32)
    slots = owners.reshape(blocks, group) * stride[:, None] + base[:, None] + position
    place = (position + offset[:, None]).reshape(-1)
    width = round_up(sum(caps), LANES)
    placed = (place[:, None] == jnp.arange(width, dtype=jnp.int32)[None, :]).astype(jnp.bfloat16)
    high = jnp.where(onehot, (rows // 128)[:, None], 0).astype(jnp.bfloat16)
    low = jnp.where(onehot, (rows % 128)[:, None], 0).astype(jnp.bfloat16)
    digits = lax.dot_general(
        jnp.concatenate([high, low], axis=1),
        placed,
        (((0,), (0,)), ((), ())),
        preferred_element_type=jnp.float32,
    )
    requests = (digits[:devices] * 128.0 + digits[devices:]).astype(jnp.int32)
    return slots.reshape(-1), requests


def greet(devices, me):
    barrier = pltpu.get_barrier_semaphore()

    def hail(step, carry):
        other = lax.rem(me + step, devices)
        pl.semaphore_signal(barrier, inc=1, device_id=(other,), device_id_type=MESH)
        return carry

    lax.fori_loop(1, devices, hail, 0)
    pl.semaphore_wait(barrier, devices - 1)


def gather_rows(table, index_of, count, staging):
    step = unroll_of(count)

    def some(turn, carry):
        for lane in range(step):
            place = turn * step + lane
            staging[pl.ds(place, 1), :] = table[pl.ds(index_of(place), 1), :]
        return carry

    lax.fori_loop(0, count // step, some, 0)


def fetch_kernel(
    devices,
    caps,
    strides,
    counts,
    requests,
    slots,
    features,
    w_first,
    w_second,
    far_kinds,
    near_kinds,
    mask,
    loss_out,
    mean_out,
    table_half,
    table,
    arrived,
    wanted,
    far_send,
    near_send,
    far_recv,
    near_recv,
    far_table,
    near_table,
    staging,
    partial,
    near_rows,
    first_hop,
    first_seed,
    second,
    part,
    seen,
    load_sem,
    small_sem,
    ask_send,
    ask_recv,
    far_send_sem,
    far_recv_sem,
    near_send_sem,
    near_recv_sem,
    tell_send,
    tell_recv,
):
    me = lax.axis_index("dom")
    far_count, first_count, seed_count = counts
    width = table.shape[1]
    far_cap, near_cap = caps
    chunk = table.shape[0] // LOADS
    loads = []
    for turn in range(LOADS):
        where = pl.ds(turn * chunk, chunk)
        loads.append(
            pltpu.make_async_copy(features.at[where], table_half.at[where], load_sem.at[turn])
        )
        loads[-1].start()
    greet(devices, me)

    def ask(turn, carry):
        other = lax.rem(me + turn * HOP, devices)
        pltpu.make_async_remote_copy(
            src_ref=requests.at[other],
            dst_ref=arrived.at[me],
            send_sem=ask_send,
            recv_sem=ask_recv,
            device_id=(other,),
            device_id_type=MESH,
        ).start()
        return carry

    lax.fori_loop(1, devices, ask, 0)
    own = pltpu.make_async_copy(requests.at[me], arrived.at[me], small_sem)
    own.start()
    part_rows = chunk // 4
    for turn in range(LOADS):
        loads[turn].wait()

        def widen(quarter, carry):
            start = pl.multiple_of(turn * chunk + quarter * part_rows, part_rows)
            where = pl.ds(start, part_rows)
            table[where, :] = table_half[where, :].astype(jnp.float32)
            return carry

        lax.fori_loop(0, 4, widen, 0)
    own.wait()
    others = pl.ds(0, devices - 1)
    pltpu.make_async_copy(requests.at[others], arrived.at[others], ask_send).wait()
    pltpu.make_async_copy(requests.at[others], arrived.at[others], ask_recv).wait()
    move = pltpu.make_async_copy(arrived, wanted, small_sem)
    move.start()
    move.wait()

    def serve(first, cap, send, recv, send_sem, recv_sem):
        def pick(other):
            gather_rows(table, lambda place: wanted[other, 0, first + place], cap, staging)
            return staging[pl.ds(0, cap), :].astype(jnp.bfloat16)

        def one(turn, carry):
            other = lax.rem(me + turn * HOP, devices)
            send[other] = pick(other)
            pltpu.make_async_remote_copy(
                src_ref=send.at[other],
                dst_ref=recv.at[me],
                send_sem=send_sem,
                recv_sem=recv_sem,
                device_id=(other,),
                device_id_type=MESH,
            ).start()
            return carry

        lax.fori_loop(1, devices, one, 0)
        recv[me] = pick(me)

    serve(0, far_cap, far_send, far_recv, far_send_sem, far_recv_sem)
    serve(far_cap, near_cap, near_send, near_recv, near_send_sem, near_recv_sem)

    def settle(send, recv, recv_sem, cap, stride, wide):
        pltpu.make_async_copy(send.at[others], recv.at[others], recv_sem).wait()

        def spread(source, carry):
            where = pl.ds(pl.multiple_of(source * stride, 8), cap)
            wide[where, :] = recv[source].astype(jnp.float32)
            return carry

        lax.fori_loop(0, devices, spread, 0)

    def weighed(values, kinds, weights):
        fan = len(values)
        hot = [
            [(kinds[:, k : k + 1] == kind).astype(jnp.float32) for k in range(fan)]
            for kind in range(R)
        ]
        result = None
        for kind in range(R):
            share = 1.0 / jnp.maximum(sum(hot[kind][1:], hot[kind][0]), 1.0)
            mean = (hot[kind][0] * share) * values[0]
            for k in range(1, fan):
                mean = mean + (hot[kind][k] * share) * values[k]
            term = jnp.dot(
                mean.astype(jnp.bfloat16),
                weights[(kind + 1) * width : (kind + 2) * width, :],
                preferred_element_type=jnp.float32,
            )
            result = term if result is None else result + term
        return result

    def itself(values, weights):
        return jnp.dot(
            values.astype(jnp.bfloat16), weights[:width, :], preferred_element_type=jnp.float32
        )

    settle(far_send, far_recv, far_recv_sem, far_cap, strides[0], far_table)

    def far_piece(turn, carry):
        start = pl.multiple_of(turn * PIECE, PIECE)
        values = []
        for k in range(FAN2):
            gather_rows(
                far_table, lambda place: slots[k * first_count + start + place], PIECE, staging
            )
            values.append(staging[pl.ds(0, PIECE), :])
        where = pl.ds(start, PIECE)
        partial[where, :] = weighed(values, far_kinds[where, :], w_first)
        return carry

    lax.fori_loop(0, first_count // PIECE, far_piece, 0)
    settle(near_send, near_recv, near_recv_sem, near_cap, strides[1], near_table)
    gather_rows(
        near_table, lambda place: slots[far_count + place], first_count + seed_count, near_rows
    )

    def hop_piece(turn, carry):
        where = pl.ds(pl.multiple_of(turn * PIECE, PIECE), PIECE)
        layer = itself(near_rows[where, :], w_first) + partial[where, :]
        rounded = jnp.maximum(layer, 0.0).astype(jnp.bfloat16)
        first_hop[where, :] = rounded.astype(jnp.float32)
        return carry

    lax.fori_loop(0, first_count // PIECE, hop_piece, 0)

    def seed_layer(start, own_rows, own_start, rows, weights):
        where = pl.ds(start, PIECE)
        values = [
            rows[pl.ds(pl.multiple_of(k * seed_count + start, PIECE), PIECE), :]
            for k in range(FAN1)
        ]
        own_where = pl.ds(pl.multiple_of(own_start + start, PIECE), PIECE)
        return itself(own_rows[own_where, :], weights) + weighed(
            values, near_kinds[where, :], weights
        )

    def seed_piece(turn, carry):
        start = pl.multiple_of(turn * PIECE, PIECE)
        where = pl.ds(start, PIECE)
        layer = seed_layer(start, near_rows, first_count, near_rows, w_first)
        first_seed[where, :] = jnp.maximum(layer, 0.0).astype(jnp.bfloat16).astype(jnp.float32)
        second[where, :] = seed_layer(start, first_seed, 0, first_hop, w_second)
        return carry

    lax.fori_loop(0, seed_count // PIECE, seed_piece, 0)

    blocks = mask.shape[0]
    positives = blocks * BLOCK
    loss_sum = jnp.zeros((1, 1), jnp.float32)
    edge_sum = jnp.zeros((1, 1), jnp.float32)

    def pairs(left, right):
        return lax.dot_general(
            left,
            right,
            (((1,), (1,)), ((), ())),
            precision=lax.Precision.HIGHEST,
            preferred_element_type=jnp.float32,
        )

    for block in range(blocks):
        sources = second[block * BLOCK : (block + 1) * BLOCK, :]
        targets = second[positives + block * BLOCK : positives + (block + 1) * BLOCK, :]
        first_neg = 2 * positives + block * NEG
        negatives = second[first_neg : first_neg + NEG, :]
        positive = pairs(jnp.ones((8, width), jnp.float32), sources * targets)[0:1, :]
        negative = pairs(negatives, sources)
        top_score = jnp.maximum(positive, jnp.max(negative, axis=0, keepdims=True))
        spread_sum = jnp.exp(positive - top_score) + jnp.sum(
            jnp.exp(negative - top_score), axis=0, keepdims=True
        )
        edge_loss = top_score + jnp.log(spread_sum) - positive
        loss_out[block : block + 1, :] = edge_loss
        counted = mask[block : block + 1, :].astype(jnp.float32)
        loss_sum = loss_sum + jnp.sum(counted * edge_loss, axis=1, keepdims=True)
        edge_sum = edge_sum + jnp.sum(counted, axis=1, keepdims=True)
    lane = lax.broadcasted_iota(jnp.int32, (1, LANES), 1)
    part[...] = jnp.where(lane == 0, loss_sum, jnp.where(lane == 1, edge_sum, 0.0))

    def tell(turn, carry):
        other = lax.rem(me + turn * HOP, devices)
        pltpu.make_async_remote_copy(
            src_ref=part,
            dst_ref=seen.at[me],
            send_sem=tell_send,
            recv_sem=tell_recv,
            device_id=(other,),
            device_id_type=MESH,
        ).start()
        return carry

    lax.fori_loop(1, devices, tell, 0)
    seen[me] = part[...]
    pltpu.make_async_copy(far_send.at[others], far_recv.at[others], far_send_sem).wait()
    pltpu.make_async_copy(near_send.at[others], near_recv.at[others], near_send_sem).wait()
    pltpu.make_async_copy(seen.at[others], seen.at[others], tell_recv).wait()
    pltpu.make_async_copy(seen.at[others], seen.at[others], tell_send).wait()
    total = jnp.sum(seen[...], axis=0)
    mean_out[...] = total[:, 0:1] / jnp.maximum(total[:, 1:2], 1.0)


def fetch(
    requests, slots, features, w_first, w_second, kinds, mask, caps, strides, counts, devices
):
    nodes, width = features.shape
    far_cap, near_cap = caps
    asked = requests.shape[1]
    half, full = jnp.bfloat16, jnp.float32
    vmem = pl.BlockSpec(memory_space=pltpu.VMEM)
    return pl.pallas_call(
        functools.partial(fetch_kernel, devices, caps, strides, counts),
        out_shape=[
            jax.ShapeDtypeStruct(mask.shape, full),
            jax.ShapeDtypeStruct((1, 1), full),
        ],
        in_specs=[
            vmem,
            pl.BlockSpec(memory_space=pltpu.SMEM),
            pl.BlockSpec(memory_space=pl.ANY),
        ]
        + [vmem] * 5,
        out_specs=[vmem, vmem],
        scratch_shapes=[
            pltpu.VMEM((nodes, width), half),
            pltpu.VMEM((nodes, width), full),
            pltpu.VMEM((devices, 1, asked), jnp.int32),
            pltpu.SMEM((devices, 1, asked), jnp.int32),
            pltpu.VMEM((devices, far_cap, width), half),
            pltpu.VMEM((devices, near_cap, width), half),
            pltpu.VMEM((devices, far_cap, width), half),
            pltpu.VMEM((devices, near_cap, width), half),
            pltpu.VMEM((devices * strides[0], width), full),
            pltpu.VMEM((devices * strides[1], width), full),
            pltpu.VMEM((round_up(max(far_cap, near_cap, PIECE), 8), width), full),
            pltpu.VMEM((counts[1], width), full),
            pltpu.VMEM((counts[1] + counts[2], width), full),
            pltpu.VMEM((counts[1], width), full),
            pltpu.VMEM((counts[2], width), full),
            pltpu.VMEM((counts[2], width), full),
            pltpu.VMEM((1, LANES), full),
            pltpu.VMEM((devices, 1, LANES), full),
        ]
        + [pltpu.SemaphoreType.DMA((LOADS,))]
        + [pltpu.SemaphoreType.DMA(())] * 9,
        compiler_params=pltpu.CompilerParams(
            collective_id=0, has_side_effects=True, vmem_limit_bytes=60 * 1024 * 1024
        ),
        name="fetch",
    )(
        requests.reshape(devices, 1, asked),
        slots,
        features,
        w_first,
        w_second,
        kinds[0],
        kinds[1],
        mask,
    )


def shards(
    features,
    w_first,
    w_second,
    seed_owner,
    seed_row,
    hop1_owner,
    hop1_row,
    hop1_rel,
    hop2_owner,
    hop2_row,
    hop2_rel,
    edge_mask,
):
    devices = lax.axis_size("dom")
    seed_count = seed_row.shape[0]
    first_count = hop1_row.shape[0]
    second_count = hop2_row.shape[0]
    caps = [
        (2 * length + devices - 1) // devices for length in (second_count, first_count, seed_count)
    ]
    near_cap = caps[1] + caps[2]
    strides = (round_up(caps[0], 8), round_up(near_cap, 8))

    def turned(values, fan):
        return values.reshape(-1, fan).T

    def hop2_order(values):
        return turned(values, FAN2).reshape(FAN2, seed_count, FAN1).swapaxes(1, 2).reshape(-1)

    def hop1_order(values):
        return turned(values, FAN1).reshape(-1)

    owners = jnp.concatenate(
        [hop2_order(hop2_owner[:, 0]), hop1_order(hop1_owner[:, 0]), seed_owner[:, 0]]
    )
    rows = jnp.concatenate([hop2_order(hop2_row), hop1_order(hop1_row), seed_row])
    sets = (second_count // seed_count, first_count // seed_count, 1)
    slots, requests = bucket_all(
        owners,
        rows,
        seed_count,
        sets,
        caps,
        (0, 0, caps[1]),
        (strides[0], strides[1], strides[1]),
        devices,
    )
    far_kinds = hop2_rel.reshape(seed_count, FAN1, FAN2).swapaxes(0, 1).reshape(-1, FAN2)
    edge_loss, mean_loss = fetch(
        requests,
        slots,
        features,
        w_first,
        w_second,
        (far_kinds, hop1_rel.reshape(seed_count, FAN1)),
        edge_mask.reshape(-1, BLOCK),
        (caps[0], near_cap),
        strides,
        (second_count, first_count, seed_count),
        devices,
    )
    return (edge_loss.reshape(-1), mean_loss[0, 0])


def solution(mesh):
    placed = (
        P("dom", None),
        P(),
        P(),
        P("dom", None),
        P("dom"),
        P("dom", None),
        P("dom"),
        P("dom"),
        P("dom", None),
        P("dom"),
        P("dom"),
        P("dom"),
    )
    return jax.shard_map(
        shards, mesh=mesh, in_specs=placed, out_specs=(P("dom"), P()), check_vma=False
    )
```

profile of v0, /device:TPU:0, one launch (start us, length us, event | category | flops | bytes accessed | tf_op | source)
XLA Modules:
  0.0 137.5 jit_solution(14328085081288824115)
XLA Ops:
  0.7 1.3 reshape.245
  1.9 0.3 copy.24
  2.2 0.1 concatenate.37
  2.3 0.9 reshape.247
  3.2 0.1 copy.25
  3.3 0.1 concatenate.38
  3.4 0.7 constant_dynamic-update-slice_fusion
  4.1 0.7 reduce
  4.8 0.5 reshape_squeeze.6
  5.4 0.3 copy.22
  5.6 0.1 reshape.243
  5.7 0.7 reduce.1
  6.5 0.2 reshape_squeeze.7
  6.6 0.1 copy.23
  6.7 0.1 reshape.244
  6.8 0.7 reduce.2
  7.5 0.1 eq.41
  7.6 0.1 convert_reduce_fusion
  7.8 0.4 fusion.4
  8.3 0.1 convert_element_type.35
  8.4 0.1 add.119
  8.6 0.1 add.123
  8.8 0.1 mul.24
  8.8 0.6 add_add_fusion
  9.4 0.1 select_convert_fusion.1
  9.5 0.8 fusion
  10.3 0.6 reshape.248.requests
  11.0 0.7 reshape.249
  11.7 0.8 copy.26
  12.5 0.8 reshape.251.near_kinds
  13.4 121.3 %fetch.1 = (f32[1,128]{1,0:T(1,128)}, f32[1,1]{1,0:T(1,128)}) custom-call(s32[32,1,256]{2,1,0:T(1,128)} %reshape.248.requests, s32[3744]{0:T(1024)} %get-tuple-element.14.slots, bf16[16384,256]{1,0:T(8,128)(2,1)} %features.1, bf16[1280,256]{1,0:T(8,128)(2,1)} %w_first.1, bf16[1280,256]{1,0:T(8,128)(2,1)} %w_second.1, s32[1152,2]{1,0:T(8,128)} %bitcast.27, ...), custom_call_target="tpu_custom_call" | custom-call | tf_op jit(solution)/shard_map/fetch/pallas_call | solution.py:358
  134.6 1.2 copy.32
  (22 shorter events, 0.4 us)
Async XLA Ops:
  0.6 7.7 %copy-start.4 = (s32[13]{0:T(128)S(1)}, s32[13]{0:T(128)}, u32[]{:S(2)}) copy-start(s32[13]{0:T(128)} %constant.40.clone) | copy-start | bytes 160
  0.6 7.9 %copy-start.3 = (s32[13]{0:T(128)S(1)}, s32[13]{0:T(128)}, u32[]{:S(2)}) copy-start(s32[13]{0:T(128)} %constant.41.clone) | copy-start | bytes 160
  0.7 8.0 %copy-start.2 = (s32[13]{0:T(128)S(1)}, s32[13]{0:T(128)}, u32[]{:S(2)}) copy-start(s32[13]{0:T(128)} %constant.42.clone) | copy-start | bytes 160
  0.7 10.3 %copy-start = (s32[2304]{0:T(1024)S(1)}, s32[2304]{0:T(1024)}, u32[]{:S(2)}) copy-start(s32[2304]{0:T(1024)} %param.25) | copy-start | bytes 27652
  5.4 7.2 %copy-start.1 = (s32[1152]{0:T(1024)S(1)}, s32[1152]{0:T(1024)}, u32[]{:S(2)}) copy-start(s32[1152]{0:T(1024)} %param.22) | copy-start | bytes 13828
where the time goes:
time: 138 us; the launch traced here: 137 us
  Pallas kernels  121 us (88%)
  local copies, waits for them, and re-layouts  9.44 us (7%)
  other arithmetic  3.06 us (2%)
  between operations  2.51 us (2%)
    pallas_call x1, Pallas kernels, fetch(): pl.pallas_call(functools.partial(fetch_kernel, devices, caps, strides, co...  121 us

commit v1 on v0

v1 whole, which is shorter than its diff:
```python
import functools

import jax
import jax.numpy as jnp
from jax import lax
from jax.experimental import pallas as pl
from jax.experimental.pallas import tpu as pltpu
from jax.sharding import PartitionSpec as P

MESH = pl.DeviceIdType.MESH
HOP = 11
PIECE = 96
LANES = 128
LOADS = 8
UNROLL = 24

R = 4
BLOCK = 128
NEG = 32
FAN1 = 4
FAN2 = 2

HALF, FULL = jnp.bfloat16, jnp.float32


def round_up(value, multiple):
    return (value + multiple - 1) // multiple * multiple


def unroll_of(count, most=UNROLL):
    return max(step for step in range(1, most + 1) if count % step == 0)


def greet(devices, me):
    barrier = pltpu.get_barrier_semaphore()

    def hail(step, carry):
        other = lax.rem(me + step, devices)
        pl.semaphore_signal(barrier, inc=1, device_id=(other,), device_id_type=MESH)
        return carry

    lax.fori_loop(1, devices, hail, 0)
    return lambda: pl.semaphore_wait(barrier, devices - 1)


def gather_rows(table, index_of, count, staging):
    step = unroll_of(count)

    def some(turn, carry):
        for lane in range(step):
            place = turn * step + lane
            staging[pl.ds(place, 1), :] = table[pl.ds(index_of(place), 1), :]
        return carry

    lax.fori_loop(0, count // step, some, 0)


def ranks(devices, owner_ref, blocks):
    lane = lax.broadcasted_iota(jnp.int32, (LANES, 2 * LANES), 1)
    item = lax.broadcasted_iota(jnp.int32, (LANES, 2 * LANES), 0)
    counting = ((item < lane) | (lane >= LANES)).astype(HALF)
    owner_id = lax.broadcasted_iota(jnp.int32, (devices, LANES), 0)
    hots = []
    for block in range(blocks):
        owner = owner_ref[0:1, block * LANES : (block + 1) * LANES]
        hots.append((owner == owner_id).astype(FULL))
    counted = jnp.dot(
        jnp.concatenate(hots, axis=0).astype(HALF), counting, preferred_element_type=FULL
    )
    running = jnp.zeros((devices, LANES), FULL)
    positions = []
    for block in range(blocks):
        mine = counted[block * devices : (block + 1) * devices]
        prior = mine[:, :LANES] + running
        running = running + mine[:, LANES:]
        positions.append(jnp.sum(prior * hots[block], axis=0, keepdims=True))
    return hots, positions


def asked_of(hots, positions, rows_ref, offset, width):
    slot = lax.broadcasted_iota(jnp.int32, (width, LANES), 0).astype(FULL)
    total = None
    for block, (hot, position) in enumerate(zip(hots, positions)):
        row = rows_ref[block : block + 1, :]
        high = lax.shift_right_logical(row, 7).astype(FULL)
        low = jnp.bitwise_and(row, 127).astype(FULL)
        digits = jnp.concatenate([hot * high, hot * low], axis=0).astype(HALF)
        placed = (slot == position + float(offset)).astype(FULL).astype(HALF)
        term = lax.dot_general(
            digits, placed, (((1,), (1,)), ((), ())), preferred_element_type=FULL
        )
        total = term if total is None else total + term
    return total


def shares_of(kinds, fan):
    first = lax.broadcasted_iota(jnp.int32, (LANES, LANES), 0) // fan
    second = lax.broadcasted_iota(jnp.int32, (LANES, LANES), 1) // fan
    together = (first == second).astype(HALF)
    count = None
    for kind in range(R):
        same = (kinds == kind).astype(FULL)
        term = same * jnp.dot(same.astype(HALF), together, preferred_element_type=FULL)
        count = term if count is None else count + term
    return 1.0 / jnp.maximum(count, 1.0)


def fetch_kernel(
    devices,
    caps,
    strides,
    counts,
    far_owner,
    first_owner,
    seed_owner,
    far_row,
    first_row,
    seed_row,
    far_kind,
    first_kind,
    features,
    w_first,
    w_second,
    near_kinds,
    mask,
    loss_out,
    mean_out,
    table_half,
    table,
    asks,
    requests,
    arrived,
    wanted,
    look_own,
    look_out,
    look_in,
    share_own,
    share_in,
    look,
    share,
    far_send,
    near_send,
    far_recv,
    near_recv,
    far_cast,
    near_cast,
    staging,
    layer,
    piece_send,
    piece_recv,
    second,
    part,
    seen,
    load_sem,
    small_sem,
    ask_send,
    ask_recv,
    info_send,
    info_recv,
    far_send_sem,
    far_recv_sem,
    near_send_sem,
    near_recv_sem,
    piece_send_sem,
    piece_recv_sem,
    tell_send,
    tell_recv,
):
    me = lax.axis_index("dom")
    side = devices // 2
    half = lax.div(me, side)
    local = lax.rem(me, side)
    mirror = lax.rem(me + side, devices)
    far_count, first_count, seed_count = counts
    width = table.shape[1]
    far_cap, first_cap, seed_cap = caps
    far_stride, near_stride = strides
    far_rows, near_rows = side * far_stride, side * near_stride
    asked = requests.shape[2]
    chunk = table.shape[0] // LOADS
    loads = []
    for turn in range(LOADS):
        where = pl.ds(turn * chunk, chunk)
        loads.append(
            pltpu.make_async_copy(features.at[where], table_half.at[where], load_sem.at[turn])
        )
        loads[-1].start()
    met = greet(devices, me)

    far_blocks, first_blocks, seed_blocks = (
        far_row.shape[0],
        first_row.shape[0],
        seed_row.shape[0],
    )
    far_hot, far_pos = ranks(devices, far_owner, far_blocks)
    first_hot, first_pos = ranks(devices, first_owner, first_blocks)
    seed_hot, seed_pos = ranks(devices, seed_owner, seed_blocks)
    digits = (
        asked_of(far_hot, far_pos, far_row, 0, asked)
        + asked_of(first_hot, first_pos, first_row, far_stride, asked)
        + asked_of(seed_hot, seed_pos, seed_row, far_stride + first_cap, asked)
    )
    wishes = (digits[:devices] * 128.0 + digits[devices:]).astype(jnp.int32)
    asks[...] = jnp.clip(wishes, 0, table.shape[0] - 1)

    def lay(owner, carry):
        requests[owner] = asks[pl.ds(owner, 1), :]
        return carry

    lax.fori_loop(0, devices, lay, 0)
    met()

    def ask(turn, carry):
        other = lax.rem(me + turn * HOP, devices)
        pltpu.make_async_remote_copy(
            src_ref=requests.at[other],
            dst_ref=arrived.at[me],
            send_sem=ask_send,
            recv_sem=ask_recv,
            device_id=(other,),
            device_id_type=MESH,
        ).start()
        return carry

    lax.fori_loop(1, devices, ask, 0)
    own_ask = pltpu.make_async_copy(requests.at[me], arrived.at[me], small_sem.at[0])
    own_ask.start()

    far_base = 0
    first_base = far_blocks * LANES
    turn_base = first_base + first_blocks * LANES
    seed_base = turn_base + first_blocks * LANES
    far_zero, near_zero = R * far_rows, (R + 1) * near_rows

    def place_of(position, cap):
        return jnp.clip(position.astype(jnp.int32), 0, cap - 1)

    def put(base, block, owner, place, kind, rows, stride, zero):
        lanes = slice(base + block * LANES, base + (block + 1) * LANES)
        for ref, whose in ((look_own, half), (look_out, 1 - half)):
            at = owner - whose * side
            held = (at >= 0) & (at < side)
            index = at * stride + place
            if kind is not None:
                index = index + kind * rows
            ref[0:1, lanes] = jnp.where(held, index, zero)

    for block in range(far_blocks):
        owner = far_owner[0:1, block * LANES : (block + 1) * LANES]
        place = place_of(far_pos[block], far_cap)
        kind = far_kind[block : block + 1, :]
        put(far_base, block, owner, place, kind, far_rows, far_stride, far_zero)
    for block in range(first_blocks):
        owner = first_owner[0:1, block * LANES : (block + 1) * LANES]
        place = place_of(first_pos[block], first_cap)
        kind = first_kind[block : block + 1, :] + 1
        put(first_base, block, owner, place, None, near_rows, near_stride, near_zero)
        put(turn_base, block, owner, place, kind, near_rows, near_stride, near_zero)
    for block in range(seed_blocks):
        owner = seed_owner[0:1, block * LANES : (block + 1) * LANES]
        place = place_of(seed_pos[block], seed_cap) + first_cap
        put(seed_base, block, owner, place, None, near_rows, near_stride, near_zero)
    far_share = shares_of(far_kind[...], FAN2)
    first_share = shares_of(first_kind[...], FAN1)
    for block in range(far_blocks):
        share_own[0:1, block * LANES : (block + 1) * LANES] = far_share[block : block + 1, :]
    for block in range(first_blocks):
        lanes = slice(first_base + block * LANES, first_base + (block + 1) * LANES)
        share_own[0:1, lanes] = first_share[block : block + 1, :]
    tells = []
    for turn, (source, target) in enumerate(((look_out, look_in), (share_own, share_in))):
        tells.append(
            pltpu.make_async_remote_copy(
                src_ref=source,
                dst_ref=target,
                send_sem=info_send.at[turn],
                recv_sem=info_recv.at[turn],
                device_id=(mirror,),
                device_id_type=MESH,
            )
        )
        tells[-1].start()
    keeps = [
        pltpu.make_async_copy(look_own, look.at[0], small_sem.at[1]),
        pltpu.make_async_copy(share_own, share.at[0], small_sem.at[2]),
    ]
    for keep in keeps:
        keep.start()

    part_rows = chunk // 4
    for turn in range(LOADS):
        loads[turn].wait()

        def widen(quarter, carry):
            start = pl.multiple_of(turn * chunk + quarter * part_rows, part_rows)
            where = pl.ds(start, part_rows)
            table[where, :] = table_half[where, :].astype(FULL)
            return carry

        lax.fori_loop(0, 4, widen, 0)
    own_ask.wait()
    others = pl.ds(0, devices - 1)
    pltpu.make_async_copy(requests.at[others], arrived.at[others], ask_send).wait()
    pltpu.make_async_copy(requests.at[others], arrived.at[others], ask_recv).wait()
    move = pltpu.make_async_copy(arrived, wanted, small_sem.at[0])
    move.start()
    move.wait()

    def serve(first, stride, send, recv, turn, send_sem, recv_sem):
        whose = lax.rem(half + turn, 2) * side
        where = pl.ds(pl.multiple_of(local * stride, stride), stride)

        def pick(other):
            gather_rows(table, lambda place: wanted[other, 0, first + place], stride, staging)
            return staging[pl.ds(0, stride), :].astype(HALF)

        def one(step, carry):
            relay = lax.rem(local + step * HOP, side)
            client = whose + relay
            send[client] = pick(client)
            pltpu.make_async_remote_copy(
                src_ref=send.at[client],
                dst_ref=recv.at[turn, where],
                send_sem=send_sem.at[turn],
                recv_sem=recv_sem.at[turn],
                device_id=(half * side + relay,),
                device_id_type=MESH,
            ).start()
            return carry

        lax.fori_loop(1, side, one, 0)
        recv[turn, where, :] = pick(whose + local)

    for turn in (1, 0):
        serve(0, far_stride, far_send, far_recv, turn, far_send_sem, far_recv_sem)
        serve(far_stride, near_stride, near_send, near_recv, turn, near_send_sem, near_recv_sem)

    far_cast[far_zero : far_zero + 8, :] = jnp.zeros((8, width), FULL)
    near_cast[near_zero : near_zero + 8, :] = jnp.zeros((8, width), FULL)

    for tell in tells:
        tell.wait()
    keeps += [
        pltpu.make_async_copy(look_in, look.at[1], small_sem.at[3]),
        pltpu.make_async_copy(share_in, share.at[1], small_sem.at[4]),
    ]
    for keep in keeps[2:]:
        keep.start()
    for keep in keeps:
        keep.wait()

    def arrive(recv, turn, rows, stride, recv_sem):
        there = pl.ds(0, rows - stride)
        block = recv.at[turn, there]
        pltpu.make_async_copy(block, block, recv_sem.at[turn]).wait()

    def project(recv, turn, rows, cast, first_kind_of, kinds):
        size = rows // 2

        def some(part_of, carry):
            start = pl.multiple_of(part_of * size, size)
            values = recv[turn, pl.ds(start, size), :]
            for kind in range(kinds):
                top = (first_kind_of + kind) * width
                target = pl.ds(pl.multiple_of(kind * rows + start, 8), size)
                cast[target, :] = jnp.dot(
                    values, w_first[top : top + width, :], preferred_element_type=FULL
                )
            return carry

        lax.fori_loop(0, 2, some, 0)

    def hop_rows(turn, fan, start, target, offset):
        step = unroll_of(PIECE, 16)

        def some(count, carry):
            for lane in range(step):
                place = count * step + lane
                item = (start + place) * FAN1 + fan
                pair = item * FAN2
                total = far_cast[pl.ds(look[turn, 0, far_base + pair], 1), :]
                for k in range(1, FAN2):
                    total = total + far_cast[pl.ds(look[turn, 0, far_base + pair + k], 1), :]
                own = near_cast[pl.ds(look[turn, 0, first_base + item], 1), :]
                target[pl.ds(offset + place, 1), :] = own + share[turn, 0, pair] * total
            return carry

        lax.fori_loop(0, PIECE // step, some, 0)

    def seed_rows(turn, start, target, offset):
        step = unroll_of(PIECE, 12)

        def some(count, carry):
            for lane in range(step):
                place = count * step + lane
                seed = start + place
                total = near_cast[pl.ds(look[turn, 0, seed_base + seed], 1), :]
                for k in range(FAN1):
                    item = seed * FAN1 + k
                    value = near_cast[pl.ds(look[turn, 0, turn_base + item], 1), :]
                    total = total + share[turn, 0, first_base + item] * value
                target[pl.ds(offset + place, 1), :] = total
            return carry

        lax.fori_loop(0, PIECE // step, some, 0)

    each = seed_count // PIECE

    def post(number):
        piece_send[number] = staging[pl.ds(0, PIECE), :].astype(HALF)
        pltpu.make_async_remote_copy(
            src_ref=piece_send.at[number],
            dst_ref=piece_recv.at[number],
            send_sem=piece_send_sem,
            recv_sem=piece_recv_sem,
            device_id=(mirror,),
            device_id_type=MESH,
        ).start()

    arrive(far_recv, 1, far_rows, far_stride, far_recv_sem)
    project(far_recv, 1, far_rows, far_cast, 1, R)
    arrive(near_recv, 1, near_rows, near_stride, near_recv_sem)
    project(near_recv, 1, near_rows, near_cast, 0, R + 1)

    def mirror_hop(number, carry):
        hop_rows(1, number // each, lax.rem(number, each) * PIECE, staging, 0)
        post(number)
        return carry

    lax.fori_loop(0, FAN1 * each, mirror_hop, 0)

    def mirror_seed(number, carry):
        seed_rows(1, number * PIECE, staging, 0)
        post(FAN1 * each + number)
        return carry

    lax.fori_loop(0, each, mirror_seed, 0)

    arrive(far_recv, 0, far_rows, far_stride, far_recv_sem)
    project(far_recv, 0, far_rows, far_cast, 1, R)
    arrive(near_recv, 0, near_rows, near_stride, near_recv_sem)
    project(near_recv, 0, near_rows, near_cast, 0, R + 1)

    def own_hop(number, carry):
        start = lax.rem(number, each) * PIECE
        hop_rows(0, number // each, start, layer, number * PIECE)
        return carry

    lax.fori_loop(0, FAN1 * each, own_hop, 0)

    def own_seed(number, carry):
        seed_rows(0, number * PIECE, layer, first_count + number * PIECE)
        return carry

    lax.fori_loop(0, each, own_seed, 0)

    pieces = (FAN1 + 1) * each
    pltpu.make_async_copy(piece_recv, piece_recv, piece_recv_sem).wait()

    def join(number, carry):
        where = pl.ds(pl.multiple_of(number * PIECE, PIECE), PIECE)
        value = jnp.maximum(layer[where, :] + piece_recv[number].astype(FULL), 0.0)
        layer[where, :] = value.astype(HALF).astype(FULL)
        return carry

    lax.fori_loop(0, pieces, join, 0)

    def weighed(values, kinds, weights):
        fan = len(values)
        hot = [
            [(kinds[:, k : k + 1] == kind).astype(FULL) for k in range(fan)] for kind in range(R)
        ]
        result = None
        for kind in range(R):
            portion = 1.0 / jnp.maximum(sum(hot[kind][1:], hot[kind][0]), 1.0)
            mean = (hot[kind][0] * portion) * values[0]
            for k in range(1, fan):
                mean = mean + (hot[kind][k] * portion) * values[k]
            term = jnp.dot(
                mean.astype(HALF),
                weights[(kind + 1) * width : (kind + 2) * width, :],
                preferred_element_type=FULL,
            )
            result = term if result is None else result + term
        return result

    def seed_piece(turn, carry):
        start = pl.multiple_of(turn * PIECE, PIECE)
        where = pl.ds(start, PIECE)
        values = [
            layer[pl.ds(pl.multiple_of(k * seed_count + start, PIECE), PIECE), :]
            for k in range(FAN1)
        ]
        own = layer[pl.ds(pl.multiple_of(first_count + start, PIECE), PIECE), :]
        second[where, :] = jnp.dot(
            own.astype(HALF), w_second[:width, :], preferred_element_type=FULL
        ) + weighed(values, near_kinds[where, :], w_second)
        return carry

    lax.fori_loop(0, each, seed_piece, 0)

    blocks = mask.shape[0]
    positives = blocks * BLOCK
    loss_sum = jnp.zeros((1, 1), FULL)
    edge_sum = jnp.zeros((1, 1), FULL)

    def pairs(left, right):
        return lax.dot_general(
            left,
            right,
            (((1,), (1,)), ((), ())),
            precision=lax.Precision.HIGHEST,
            preferred_element_type=FULL,
        )

    for block in range(blocks):
        sources = second[block * BLOCK : (block + 1) * BLOCK, :]
        targets = second[positives + block * BLOCK : positives + (block + 1) * BLOCK, :]
        first_neg = 2 * positives + block * NEG
        negatives = second[first_neg : first_neg + NEG, :]
        positive = pairs(jnp.ones((8, width), FULL), sources * targets)[0:1, :]
        negative = pairs(negatives, sources)
        top_score = jnp.maximum(positive, jnp.max(negative, axis=0, keepdims=True))
        spread_sum = jnp.exp(positive - top_score) + jnp.sum(
            jnp.exp(negative - top_score), axis=0, keepdims=True
        )
        edge_loss = top_score + jnp.log(spread_sum) - positive
        loss_out[block : block + 1, :] = edge_loss
        counted = mask[block : block + 1, :].astype(FULL)
        loss_sum = loss_sum + jnp.sum(counted * edge_loss, axis=1, keepdims=True)
        edge_sum = edge_sum + jnp.sum(counted, axis=1, keepdims=True)
    lane = lax.broadcasted_iota(jnp.int32, (1, LANES), 1)
    part[...] = jnp.where(lane == 0, loss_sum, jnp.where(lane == 1, edge_sum, 0.0))

    def tell_all(turn, carry):
        other = lax.rem(me + turn * HOP, devices)
        pltpu.make_async_remote_copy(
            src_ref=part,
            dst_ref=seen.at[me],
            send_sem=tell_send,
            recv_sem=tell_recv,
            device_id=(other,),
            device_id_type=MESH,
        ).start()
        return carry

    lax.fori_loop(1, devices, tell_all, 0)
    seen[me] = part[...]
    near_side = pl.ds(0, side - 1)
    for turn in range(2):
        sent = far_send.at[near_side]
        pltpu.make_async_copy(sent, sent, far_send_sem.at[turn]).wait()
        sent = near_send.at[near_side]
        pltpu.make_async_copy(sent, sent, near_send_sem.at[turn]).wait()
    pltpu.make_async_copy(piece_send, piece_send, piece_send_sem).wait()
    pltpu.make_async_copy(seen.at[others], seen.at[others], tell_recv).wait()
    pltpu.make_async_copy(seen.at[others], seen.at[others], tell_send).wait()
    total = jnp.sum(seen[...], axis=0)
    mean_out[...] = total[:, 0:1] / jnp.maximum(total[:, 1:2], 1.0)


def fetch(owners, rows, kinds, features, w_first, w_second, near_kinds, mask, caps, counts, devices):
    nodes, width = features.shape
    side = devices // 2
    strides = (round_up(caps[0], 16), round_up(caps[1] + caps[2], 16))
    asked = round_up(sum(strides), LANES)
    far_rows, near_rows = side * strides[0], side * strides[1]
    looks = LANES * (rows[0].shape[0] + 2 * rows[1].shape[0] + rows[2].shape[0])
    shared = LANES * (rows[0].shape[0] + rows[1].shape[0])
    pieces = (counts[1] + counts[2]) // PIECE
    number = jnp.int32
    vmem = pl.BlockSpec(memory_space=pltpu.VMEM)
    return pl.pallas_call(
        functools.partial(fetch_kernel, devices, caps, strides, counts),
        out_shape=[
            jax.ShapeDtypeStruct(mask.shape, FULL),
            jax.ShapeDtypeStruct((1, 1), FULL),
        ],
        in_specs=[vmem] * 8 + [pl.BlockSpec(memory_space=pl.ANY)] + [vmem] * 4,
        out_specs=[vmem, vmem],
        scratch_shapes=[
            pltpu.VMEM((nodes, width), HALF),
            pltpu.VMEM((nodes, width), FULL),
            pltpu.VMEM((devices, asked), number),
            pltpu.VMEM((devices, 1, asked), number),
            pltpu.VMEM((devices, 1, asked), number),
            pltpu.SMEM((devices, 1, asked), number),
            pltpu.VMEM((1, looks), number),
            pltpu.VMEM((1, looks), number),
            pltpu.VMEM((1, looks), number),
            pltpu.VMEM((1, shared), FULL),
            pltpu.VMEM((1, shared), FULL),
            pltpu.SMEM((2, 1, looks), number),
            pltpu.SMEM((2, 1, shared), FULL),
            pltpu.VMEM((devices, strides[0], width), HALF),
            pltpu.VMEM((devices, strides[1], width), HALF),
            pltpu.VMEM((2, far_rows, width), HALF),
            pltpu.VMEM((2, near_rows, width), HALF),
            pltpu.VMEM((R * far_rows + 8, width), FULL),
            pltpu.VMEM(((R + 1) * near_rows + 8, width), FULL),
            pltpu.VMEM((round_up(max(strides[0], strides[1], PIECE), 8), width), FULL),
            pltpu.VMEM((counts[1] + counts[2], width), FULL),
            pltpu.VMEM((pieces, PIECE, width), HALF),
            pltpu.VMEM((pieces, PIECE, width), HALF),
            pltpu.VMEM((counts[2], width), FULL),
            pltpu.VMEM((1, LANES), FULL),
            pltpu.VMEM((devices, 1, LANES), FULL),
            pltpu.SemaphoreType.DMA((LOADS,)),
            pltpu.SemaphoreType.DMA((5,)),
            pltpu.SemaphoreType.DMA(()),
            pltpu.SemaphoreType.DMA(()),
        ]
        + [pltpu.SemaphoreType.DMA((2,))] * 6
        + [pltpu.SemaphoreType.DMA(())] * 4,
        compiler_params=pltpu.CompilerParams(
            collective_id=0, has_side_effects=True, vmem_limit_bytes=67043328
        ),
        name="fetch",
    )(*owners, *rows, *kinds, features, w_first, w_second, near_kinds, mask)


def shards(
    features,
    w_first,
    w_second,
    seed_owner,
    seed_row,
    hop1_owner,
    hop1_row,
    hop1_rel,
    hop2_owner,
    hop2_row,
    hop2_rel,
    edge_mask,
):
    devices = lax.axis_size("dom")
    counts = (hop2_row.shape[0], hop1_row.shape[0], seed_row.shape[0])
    caps = tuple((2 * length + devices - 1) // devices for length in counts)

    def flat(values, filler):
        length = values.shape[0]
        values = values.reshape(1, length)
        spare = round_up(length, LANES) - length
        return jnp.pad(values, ((0, 0), (0, spare)), constant_values=filler) if spare else values

    def stacked(values):
        length = values.shape[0]
        spare = round_up(length, LANES) - length
        values = jnp.pad(values, (0, spare)) if spare else values
        return values.reshape(-1, LANES)

    edge_loss, mean_loss = fetch(
        [flat(owner, -1) for owner in (hop2_owner, hop1_owner, seed_owner)],
        [stacked(row) for row in (hop2_row, hop1_row, seed_row)],
        [stacked(rel) for rel in (hop2_rel, hop1_rel)],
        features,
        w_first,
        w_second,
        hop1_rel.reshape(-1, FAN1),
        edge_mask.reshape(-1, BLOCK),
        caps,
        counts,
        devices,
    )
    return (edge_loss.reshape(-1), mean_loss[0, 0])


def solution(mesh):
    placed = (
        P("dom", None),
        P(),
        P(),
        P("dom", None),
        P("dom"),
        P("dom", None),
        P("dom"),
        P("dom"),
        P("dom", None),
        P("dom"),
        P("dom"),
        P("dom"),
    )
    return jax.shard_map(
        shards, mesh=mesh, in_specs=placed, out_specs=(P("dom"), P()), check_vma=False
    )
```

time: 138 us -> 113 us (0.82)
  Pallas kernels: 121 us -> 106 us
  local copies, waits for them, and re-layouts: 9.44 us -> 5.19 us
  other arithmetic: 3.06 us -> 0 us
    pallas_call x1, Pallas kernels: 121 us -> 106 us  [fetch(): pl.pallas_call(functools.partial(fetch_kernel, devices, caps, strides, co...]
    reshape x9 -> x2, local copies, waits for them, and re-layouts: 4.97 us -> 2.75 us  [the longest x1 1.5 us: shards(): hop1_rel.reshape(-1, FAN1)]
    unnamed x4 -> x0, other arithmetic: 2.18 us -> none
where the time goes in v1:
time: 113 us
  Pallas kernels  106 us (94%)
  local copies, waits for them, and re-layouts  5.19 us (5%)
  between operations  2.4 us (2%)
    pallas_call x1, Pallas kernels, fetch(): pl.pallas_call(functools.partial(fetch_kernel, devices, caps, strides, co...  106 us

profile of v1, /device:TPU:0, one launch (start us, length us, event | category | flops | bytes accessed | tf_op | source)
XLA Modules:
  0.0 113.1 jit_solution(3357344587239418093)
XLA Ops:
  0.6 1.3 %pad.8.seed_owner = s32[1,384]{1,0:T(1,128)} pad(s32[1,288]{1,0:T(1,128)} %bitcast.18, s32[]{:T(128)} %constant.0.clone.1), padding=0_0x0_96 | pad | bytes 2692 | tf_op jit(solution)/shard_map/jit(_pad)/pad | solution.py:644
  1.9 1.2 %pad_bitcast_fusion.seed_row = s32[3,128]{1,0:T(4,128)} fusion(s32[288]{0:T(512)} %param.16), kind=kLoop, calls=%fused_computation | loop fusion | bytes 2688 | tf_op jit(solution)/shard_map/reshape | solution.py:650
  3.1 1.5 %reshape.45.near_kinds = s32[288,4]{1,0:T(8,128)} reshape(s32[1152]{0:T(1024)} %param.19) | data formatting | bytes 9216 | tf_op jit(solution)/shard_map/reshape | solution.py:659
  4.6 105.5 %fetch.1 = (f32[1,128]{1,0:T(1,128)}, f32[1,1]{1,0:T(1,128)}) custom-call(s32[1,2304]{1,0:T(1,128)} %bitcast.15, s32[1,1152]{1,0:T(1,128)} %bitcast.17, s32[1,384]{1,0:T(1,128)} %pad.8.seed_owner, s32[18,128]{1,0:T(8,128)} %bitcast.13, s32[9,128]{1,0:T(8,128)} %bitcast.16, s32[3,128]{1,0:T(4,128)} %pad_bitcast_fusion.seed_row, s32[18,128]{1,0:T(8,128)} %bitcast.14, ...), custom_call_target="tpu_custom_call" | custom-call | tf_op jit(solution)/shard_map/fetch/pallas_call | solution.py:573
  110.2 1.2 %copy.16 = f32[128]{0:T(128)} copy(f32[128]{0:T(128)} %bitcast.20) | data formatting | bytes 1024

commit v2 on v1

v2 whole, which is shorter than its diff:
```python
import functools

import jax
import jax.numpy as jnp
from jax import lax
from jax.experimental import pallas as pl
from jax.experimental.pallas import tpu as pltpu
from jax.sharding import PartitionSpec as P

MESH = pl.DeviceIdType.MESH
HOP = 11
ROWS = 96
LANES = 128
LOADS = 8
SLOTS = 4

R = 4
BLOCK = 128
NEG = 32
FAN1 = 4
FAN2 = 2

HALF, FULL = jnp.bfloat16, jnp.float32


def round_up(value, multiple):
    return (value + multiple - 1) // multiple * multiple


def paired(ref, start, count):
    parts = [ref[pl.ds(start + part, count, stride=2), :] for part in range(2)]
    return jnp.concatenate(parts, axis=1)


def pair_up(ref, start, values):
    count = values.shape[0]
    for part in range(2):
        ref[pl.ds(start + part, count, stride=2), :] = values[:, part * LANES : (part + 1) * LANES]


def greet(devices, me):
    barrier = pltpu.get_barrier_semaphore()

    def hail(step, carry):
        other = lax.rem(me + step, devices)
        pl.semaphore_signal(barrier, inc=1, device_id=(other,), device_id_type=MESH)
        return carry

    lax.fori_loop(1, devices, hail, 0)
    return lambda: pl.semaphore_wait(barrier, devices - 1)


def ranks(devices, owner_ref, blocks):
    lane = lax.broadcasted_iota(jnp.int32, (LANES, 2 * LANES), 1)
    item = lax.broadcasted_iota(jnp.int32, (LANES, 2 * LANES), 0)
    counting = ((item < lane) | (lane >= LANES)).astype(HALF)
    owner_id = lax.broadcasted_iota(jnp.int32, (devices, LANES), 0)
    hots = []
    for block in range(blocks):
        owner = owner_ref[0:1, block * LANES : (block + 1) * LANES]
        hots.append((owner == owner_id).astype(FULL))
    counted = jnp.dot(
        jnp.concatenate(hots, axis=0).astype(HALF), counting, preferred_element_type=FULL
    )
    running = jnp.zeros((devices, LANES), FULL)
    positions = []
    for block in range(blocks):
        mine = counted[block * devices : (block + 1) * devices]
        prior = mine[:, :LANES] + running
        running = running + mine[:, LANES:]
        positions.append(jnp.sum(prior * hots[block], axis=0, keepdims=True))
    return hots, positions


def asked_of(hots, positions, rows, offset, width):
    slot = lax.broadcasted_iota(jnp.int32, (width, LANES), 0).astype(FULL)
    total = None
    for block, (hot, position) in enumerate(zip(hots, positions)):
        row = rows[block]
        high = lax.shift_right_logical(row, 7).astype(FULL)
        low = jnp.bitwise_and(row, 127).astype(FULL)
        digits = jnp.concatenate([hot * high, hot * low], axis=0).astype(HALF)
        placed = (slot == position + float(offset)).astype(FULL).astype(HALF)
        term = lax.dot_general(
            digits, placed, (((1,), (1,)), ((), ())), preferred_element_type=FULL
        )
        total = term if total is None else total + term
    return total


def shares_of(kinds, fan):
    first = lax.broadcasted_iota(jnp.int32, (LANES, LANES), 0) // fan
    second = lax.broadcasted_iota(jnp.int32, (LANES, LANES), 1) // fan
    together = (first == second).astype(HALF)
    count = None
    for kind in range(R):
        same = (kinds == kind).astype(FULL)
        term = same * jnp.dot(same.astype(HALF), together, preferred_element_type=FULL)
        count = term if count is None else count + term
    return 1.0 / jnp.maximum(count, 1.0)


def fetch_kernel(
    devices,
    caps,
    strides,
    counts,
    far_owner,
    first_owner,
    seed_owner,
    far_row,
    first_row,
    seed_row,
    far_kind,
    first_kind,
    features,
    w_first,
    w_second,
    mask,
    loss_out,
    mean_out,
    first_weights,
    second_weights,
    spare_owner,
    spare_row,
    table_half,
    table,
    asks,
    requests,
    arrived,
    wanted,
    look_own,
    look_out,
    look_in,
    share_own,
    share_in,
    look,
    share,
    far_send,
    near_send,
    far_recv,
    near_recv,
    far_cast,
    near_cast,
    staging,
    mine,
    hop_layer,
    seed_input,
    kind_columns,
    piece_send,
    piece_recv,
    second,
    part,
    seen,
    load_sem,
    weight_sem,
    small_sem,
    ask_send,
    ask_recv,
    info_send,
    info_recv,
    far_send_sem,
    far_recv_sem,
    near_send_sem,
    near_recv_sem,
    piece_send_sem,
    piece_recv_sem,
    tell_send,
    tell_recv,
):
    me = lax.axis_index("dom")
    side = devices // 2
    half = lax.div(me, side)
    local = lax.rem(me, side)
    mirror = lax.rem(me + side, devices)
    far_count, first_count, seed_count = counts
    width = features.shape[1]
    far_cap, first_cap, seed_cap = caps
    far_stride, near_stride = strides
    far_rows, near_rows = side * far_stride, side * near_stride
    asked = requests.shape[2]
    nodes = features.shape[0]
    chunk = nodes // LOADS
    loads = [
        pltpu.make_async_copy(
            features.at[pl.ds(turn * chunk, chunk)],
            table_half.at[turn % SLOTS],
            load_sem.at[turn],
        )
        for turn in range(LOADS)
    ]
    for load in loads[:SLOTS]:
        load.start()
    weigh = [
        pltpu.make_async_copy(w_first, first_weights, weight_sem.at[0]),
        pltpu.make_async_copy(w_second, second_weights, weight_sem.at[1]),
    ]
    for copy in weigh:
        copy.start()
    met = greet(devices, me)

    spare_owner[...] = jnp.full(spare_owner.shape, -1, jnp.int32)
    spare_row[...] = jnp.zeros(spare_row.shape, jnp.int32)
    spare_owner[0:1, 0:seed_count] = seed_owner[...]
    spare_row[0:1, 0:seed_count] = seed_row[...]
    far_blocks, first_blocks = far_row.shape[0], first_row.shape[0]
    seed_blocks = spare_row.shape[1] // LANES
    lanes_of = [slice(block * LANES, (block + 1) * LANES) for block in range(far_blocks)]
    far_hot, far_pos = ranks(devices, far_owner, far_blocks)
    first_hot, first_pos = ranks(devices, first_owner, first_blocks)
    seed_hot, seed_pos = ranks(devices, spare_owner, seed_blocks)
    far_rows_of = [far_row[block : block + 1, :] for block in range(far_blocks)]
    first_rows_of = [first_row[block : block + 1, :] for block in range(first_blocks)]
    seed_rows_of = [spare_row[0:1, lanes_of[block]] for block in range(seed_blocks)]
    digits = (
        asked_of(far_hot, far_pos, far_rows_of, 0, asked)
        + asked_of(first_hot, first_pos, first_rows_of, far_stride, asked)
        + asked_of(seed_hot, seed_pos, seed_rows_of, far_stride + first_cap, asked)
    )
    wishes = (digits[:devices] * 128.0 + digits[devices:]).astype(jnp.int32)
    asks[...] = jnp.clip(wishes, 0, nodes - 1) * 2

    def lay(owner, carry):
        requests[owner] = asks[pl.ds(owner, 1), :]
        return carry

    lax.fori_loop(0, devices, lay, 0)
    met()

    def ask(turn, carry):
        other = lax.rem(me + turn * HOP, devices)
        pltpu.make_async_remote_copy(
            src_ref=requests.at[other],
            dst_ref=arrived.at[me],
            send_sem=ask_send,
            recv_sem=ask_recv,
            device_id=(other,),
            device_id_type=MESH,
        ).start()
        return carry

    lax.fori_loop(1, devices, ask, 0)
    own_ask = pltpu.make_async_copy(requests.at[me], arrived.at[me], small_sem.at[0])
    own_ask.start()

    first_base = far_blocks
    turn_base = first_base + first_blocks
    seed_base = turn_base + first_blocks
    looks, shared = seed_base + first_blocks, far_blocks + first_blocks
    seed_lanes = LANES // FAN1
    far_zero, near_zero = R * far_rows, (R + 1) * near_rows

    def place_of(position, cap):
        return jnp.clip(position.astype(jnp.int32), 0, cap - 1)

    def put(owner, place, kind, rows, stride, zero, store):
        for ref, whose in ((look_own, half), (look_out, 1 - half)):
            at = owner - whose * side
            held = (at >= 0) & (at < side)
            index = at * stride + place
            if kind is not None:
                index = index + kind * rows
            store(ref, jnp.where(held, index, zero) * 2)

    def at_row(row):
        def store(ref, value):
            ref[row] = value

        return store

    def at_seeds(block):
        def store(ref, value):
            for turn in range(FAN1):
                row = block * FAN1 + turn
                if row < first_blocks:
                    lanes = slice(turn * seed_lanes, (turn + 1) * seed_lanes)
                    ref[seed_base + row, 0:1, 0:seed_lanes] = value[:, lanes]

        return store

    for block in range(far_blocks):
        owner = far_owner[0:1, lanes_of[block]]
        place = place_of(far_pos[block], far_cap)
        kind = far_kind[block : block + 1, :]
        put(owner, place, kind, far_rows, far_stride, far_zero, at_row(block))
    for block in range(first_blocks):
        owner = first_owner[0:1, lanes_of[block]]
        place = place_of(first_pos[block], first_cap)
        kind = first_kind[block : block + 1, :] + 1
        put(owner, place, None, near_rows, near_stride, near_zero, at_row(first_base + block))
        put(owner, place, kind, near_rows, near_stride, near_zero, at_row(turn_base + block))
    for block in range(seed_blocks):
        owner = spare_owner[0:1, lanes_of[block]]
        place = place_of(seed_pos[block], seed_cap) + first_cap
        put(owner, place, None, near_rows, near_stride, near_zero, at_seeds(block))
    far_share = shares_of(far_kind[...], FAN2)
    first_share = shares_of(first_kind[...], FAN1)
    for block in range(far_blocks):
        share_own[block] = far_share[block : block + 1, :]
    for block in range(first_blocks):
        share_own[far_blocks + block] = first_share[block : block + 1, :]
    tells = []
    for turn, (source, target) in enumerate(((look_out, look_in), (share_own, share_in))):
        tells.append(
            pltpu.make_async_remote_copy(
                src_ref=source,
                dst_ref=target,
                send_sem=info_send.at[turn],
                recv_sem=info_recv.at[turn],
                device_id=(mirror,),
                device_id_type=MESH,
            )
        )
        tells[-1].start()
    keeps = [
        pltpu.make_async_copy(look_own, look.at[pl.ds(0, looks)], small_sem.at[1]),
        pltpu.make_async_copy(share_own, share.at[pl.ds(0, shared)], small_sem.at[2]),
    ]
    for keep in keeps:
        keep.start()

    part_rows = chunk // 4
    for turn in range(LOADS):
        loads[turn].wait()

        def widen(quarter, carry):
            start = pl.multiple_of(quarter * part_rows, part_rows)
            values = table_half[turn % SLOTS, pl.ds(start, part_rows), :].astype(FULL)
            pair_up(table, pl.multiple_of(2 * (turn * chunk + start), 8), values)
            return carry

        lax.fori_loop(0, 4, widen, 0)
        if turn + SLOTS < LOADS:
            loads[turn + SLOTS].start()
    own_ask.wait()
    others = pl.ds(0, devices - 1)
    pltpu.make_async_copy(requests.at[others], arrived.at[others], ask_send).wait()
    pltpu.make_async_copy(requests.at[others], arrived.at[others], ask_recv).wait()
    move = pltpu.make_async_copy(arrived, wanted, small_sem.at[0])
    move.start()
    move.wait()

    def serve(turn):
        whose = lax.rem(half + turn, 2) * side
        parts = (
            (0, far_stride, far_send, far_recv, far_send_sem, far_recv_sem),
            (far_stride, near_stride, near_send, near_recv, near_send_sem, near_recv_sem),
        )

        def one(step, carry):
            relay = lax.rem(local + step * HOP, side)
            client = whose + relay
            for first, stride, send, recv, send_sem, recv_sem in parts:
                for place in range(first, first + stride):
                    row = table[pl.ds(wanted[client, 0, place], 2), :]
                    staging[2 * place : 2 * place + 2, :] = row
                send[client] = paired(staging, 2 * first, stride).astype(HALF)
                where = pl.ds(pl.multiple_of(local * stride, stride), stride)

                @pl.when(step < side)
                def _():
                    pltpu.make_async_remote_copy(
                        src_ref=send.at[client],
                        dst_ref=recv.at[turn, where],
                        send_sem=send_sem.at[turn],
                        recv_sem=recv_sem.at[turn],
                        device_id=(half * side + relay,),
                        device_id_type=MESH,
                    ).start()

                @pl.when(step == side)
                def _():
                    recv[turn, where, :] = send[client]

            return carry

        lax.fori_loop(1, side + 1, one, 0)

    serve(1)
    serve(0)

    far_cast[2 * far_zero : 2 * far_zero + 8, :] = jnp.zeros((8, LANES), FULL)
    near_cast[2 * near_zero : 2 * near_zero + 8, :] = jnp.zeros((8, LANES), FULL)

    lane = lax.broadcasted_iota(jnp.int32, (1, LANES), 1)
    seed_of = lax.broadcasted_iota(jnp.int32, (seed_lanes, LANES), 1) // FAN1
    chosen = (seed_of == lax.broadcasted_iota(jnp.int32, (seed_lanes, LANES), 0)).astype(HALF)
    for block in range(first_blocks):
        kinds = first_kind[block : block + 1, :]
        hot = [
            ((kinds == kind) & (lane % FAN1 == k)).astype(FULL)
            for k in range(FAN1)
            for kind in range(R)
        ]
        kind_columns[block * seed_lanes : (block + 1) * seed_lanes, 0 : FAN1 * R] = lax.dot_general(
            chosen,
            jnp.concatenate(hot, axis=0).astype(HALF),
            (((1,), (1,)), ((), ())),
            preferred_element_type=FULL,
        )

    for copy in weigh:
        copy.wait()
    for tell in tells:
        tell.wait()
    keeps += [
        pltpu.make_async_copy(look_in, look.at[pl.ds(looks, looks)], small_sem.at[3]),
        pltpu.make_async_copy(share_in, share.at[pl.ds(shared, shared)], small_sem.at[4]),
    ]
    for keep in keeps[2:]:
        keep.start()
    for keep in keeps:
        keep.wait()

    def arrive(recv, turn, rows, stride, recv_sem):
        there = pl.ds(0, rows - stride)
        block = recv.at[turn, there]
        pltpu.make_async_copy(block, block, recv_sem.at[turn]).wait()

    def project(recv, turn, rows, cast, first_kind_of, kinds):
        size = rows // 2

        def some(part_of, carry):
            start = pl.multiple_of(part_of * size, size)
            values = recv[turn, pl.ds(start, size), :]
            for kind in range(kinds):
                top = (first_kind_of + kind) * width
                term = jnp.dot(
                    values, first_weights[top : top + width, :], preferred_element_type=FULL
                )
                pair_up(cast, pl.multiple_of(2 * (kind * rows + start), 8), term)
            return carry

        lax.fori_loop(0, 2, some, 0)

    def sums(turn, block, target):
        look_row, share_row = turn * looks, turn * shared

        def at(cast, row, lane_of):
            return cast[pl.ds(look[look_row + row, 0, lane_of], 2), :]

        for item in range(LANES):
            row, first = (item * FAN2) // LANES, (item * FAN2) % LANES
            total = at(far_cast, block * FAN2 + row, first)
            for k in range(1, FAN2):
                total = total + at(far_cast, block * FAN2 + row, first + k)
            scale = share[share_row + block * FAN2 + row, 0, first]
            target[2 * item : 2 * item + 2, :] = (
                at(near_cast, first_base + block, item) + scale * total
            )
        for seed in range(seed_lanes):
            total = at(near_cast, seed_base + block, seed)
            for k in range(FAN1):
                item = seed * FAN1 + k
                scale = share[share_row + far_blocks + block, 0, item]
                total = total + scale * at(near_cast, turn_base + block, item)
            place = 2 * (LANES + seed)
            target[place : place + 2, :] = total

    piece = LANES + seed_lanes
    arrive(far_recv, 1, far_rows, far_stride, far_recv_sem)
    project(far_recv, 1, far_rows, far_cast, 1, R)
    arrive(near_recv, 1, near_rows, near_stride, near_recv_sem)
    project(near_recv, 1, near_rows, near_cast, 0, R + 1)

    def mirror_block(block, carry):
        sums(1, block, staging)
        piece_send[block] = paired(staging, 0, piece).astype(HALF)
        pltpu.make_async_remote_copy(
            src_ref=piece_send.at[block],
            dst_ref=piece_recv.at[block],
            send_sem=piece_send_sem,
            recv_sem=piece_recv_sem,
            device_id=(mirror,),
            device_id_type=MESH,
        ).start()
        return carry

    lax.fori_loop(0, first_blocks, mirror_block, 0)

    arrive(far_recv, 0, far_rows, far_stride, far_recv_sem)
    project(far_recv, 0, far_rows, far_cast, 1, R)
    arrive(near_recv, 0, near_rows, near_stride, near_recv_sem)
    project(near_recv, 0, near_rows, near_cast, 0, R + 1)

    def own_block(block, carry):
        sums(0, block, staging)
        mine[block] = paired(staging, 0, piece)
        return carry

    lax.fori_loop(0, first_blocks, own_block, 0)

    pltpu.make_async_copy(piece_recv, piece_recv, piece_recv_sem).wait()

    def join(block, carry):
        value = jnp.maximum(mine[block] + piece_recv[block].astype(FULL), 0.0).astype(HALF)
        hops = pl.ds(pl.multiple_of(block * LANES, LANES), LANES)
        for part_of in range(2):
            hop_layer[part_of, hops, :] = value[:LANES, lanes_of[part_of]].astype(FULL)
        seeds = pl.ds(pl.multiple_of(block * seed_lanes, seed_lanes), seed_lanes)
        seed_input[seeds, 0:width] = value[LANES:]
        return carry

    lax.fori_loop(0, first_blocks, join, 0)

    def means(turn, carry):
        start = pl.multiple_of(turn * ROWS, ROWS)
        where = pl.ds(start, ROWS)
        values = [
            jnp.concatenate(
                [
                    hop_layer[part_of, pl.ds(start * FAN1 + k, ROWS, stride=FAN1), :]
                    for part_of in range(2)
                ],
                axis=1,
            )
            for k in range(FAN1)
        ]
        columns = kind_columns[where, :]
        for kind in range(R):
            hot = [columns[:, k * R + kind : k * R + kind + 1] for k in range(FAN1)]
            portion = 1.0 / jnp.maximum(sum(hot[1:], hot[0]), 1.0)
            mean = (hot[0] * portion) * values[0]
            for k in range(1, FAN1):
                mean = mean + (hot[k] * portion) * values[k]
            seed_input[where, (kind + 1) * width : (kind + 2) * width] = mean.astype(HALF)
        return carry

    lax.fori_loop(0, seed_count // ROWS, means, 0)
    second[...] = jnp.dot(seed_input[...], second_weights[...], preferred_element_type=FULL)

    blocks = mask.shape[0]
    positives = blocks * BLOCK
    loss_sum = jnp.zeros((1, 1), FULL)
    edge_sum = jnp.zeros((1, 1), FULL)

    diagonal = lax.broadcasted_iota(jnp.int32, (BLOCK, BLOCK), 0) == lax.broadcasted_iota(
        jnp.int32, (BLOCK, BLOCK), 1
    )
    for block in range(blocks):
        sources = second[block * BLOCK : (block + 1) * BLOCK, :]
        targets = second[positives + block * BLOCK : positives + (block + 1) * BLOCK, :]
        first_neg = 2 * positives + block * NEG
        negatives = second[first_neg : first_neg + NEG, :]
        scores = lax.dot_general(
            jnp.concatenate([targets, negatives], axis=0),
            sources,
            (((1,), (1,)), ((), ())),
            precision=lax.Precision.HIGHEST,
            preferred_element_type=FULL,
        )
        positive = jnp.sum(jnp.where(diagonal, scores[:BLOCK], 0.0), axis=0, keepdims=True)
        negative = scores[BLOCK:]
        top_score = jnp.maximum(positive, jnp.max(negative, axis=0, keepdims=True))
        spread_sum = jnp.exp(positive - top_score) + jnp.sum(
            jnp.exp(negative - top_score), axis=0, keepdims=True
        )
        edge_loss = top_score + jnp.log(spread_sum) - positive
        loss_out[block : block + 1, :] = edge_loss
        counted = mask[block : block + 1, :].astype(FULL)
        loss_sum = loss_sum + jnp.sum(counted * edge_loss, axis=1, keepdims=True)
        edge_sum = edge_sum + jnp.sum(counted, axis=1, keepdims=True)
    part[...] = jnp.where(lane == 0, loss_sum, jnp.where(lane == 1, edge_sum, 0.0))

    def tell_all(turn, carry):
        other = lax.rem(me + turn * HOP, devices)
        pltpu.make_async_remote_copy(
            src_ref=part,
            dst_ref=seen.at[me],
            send_sem=tell_send,
            recv_sem=tell_recv,
            device_id=(other,),
            device_id_type=MESH,
        ).start()
        return carry

    lax.fori_loop(1, devices, tell_all, 0)
    seen[me] = part[...]
    near_side = pl.ds(0, side - 1)
    for turn in range(2):
        sent = far_send.at[near_side]
        pltpu.make_async_copy(sent, sent, far_send_sem.at[turn]).wait()
        sent = near_send.at[near_side]
        pltpu.make_async_copy(sent, sent, near_send_sem.at[turn]).wait()
    pltpu.make_async_copy(piece_send, piece_send, piece_send_sem).wait()
    pltpu.make_async_copy(seen.at[others], seen.at[others], tell_recv).wait()
    pltpu.make_async_copy(seen.at[others], seen.at[others], tell_send).wait()
    total = jnp.sum(seen[...], axis=0)
    mean_out[...] = total[:, 0:1] / jnp.maximum(total[:, 1:2], 1.0)


def fetch(owners, rows, kinds, features, w_first, w_second, mask, caps, counts, devices):
    nodes, width = features.shape
    side = devices // 2
    strides = (round_up(caps[0], 16), round_up(caps[1] + caps[2], 16))
    asked = round_up(sum(strides), LANES)
    far_rows, near_rows = side * strides[0], side * strides[1]
    far_blocks, first_blocks = rows[0].shape[0], rows[1].shape[0]
    looks, shared = far_blocks + 3 * first_blocks, far_blocks + first_blocks
    piece = LANES + LANES // FAN1
    number = jnp.int32
    vmem, anywhere = (pl.BlockSpec(memory_space=space) for space in (pltpu.VMEM, pl.ANY))
    return pl.pallas_call(
        functools.partial(fetch_kernel, devices, caps, strides, counts),
        out_shape=[
            jax.ShapeDtypeStruct(mask.shape, FULL),
            jax.ShapeDtypeStruct((1, 1), FULL),
        ],
        in_specs=[vmem] * 8 + [anywhere] * 3 + [vmem],
        out_specs=[vmem, vmem],
        scratch_shapes=[
            pltpu.VMEM(w_first.shape, HALF),
            pltpu.VMEM(w_second.shape, HALF),
            pltpu.VMEM((1, round_up(counts[2], LANES)), number),
            pltpu.VMEM((1, round_up(counts[2], LANES)), number),
            pltpu.VMEM((SLOTS, nodes // LOADS, width), HALF),
            pltpu.VMEM((2 * nodes, LANES), FULL),
            pltpu.VMEM((devices, asked), number),
            pltpu.VMEM((devices, 1, asked), number),
            pltpu.VMEM((devices, 1, asked), number),
            pltpu.SMEM((devices, 1, asked), number),
            pltpu.VMEM((looks, 1, LANES), number),
            pltpu.VMEM((looks, 1, LANES), number),
            pltpu.VMEM((looks, 1, LANES), number),
            pltpu.VMEM((shared, 1, LANES), FULL),
            pltpu.VMEM((shared, 1, LANES), FULL),
            pltpu.SMEM((2 * looks, 1, LANES), number),
            pltpu.SMEM((2 * shared, 1, LANES), FULL),
            pltpu.VMEM((devices, strides[0], width), HALF),
            pltpu.VMEM((devices, strides[1], width), HALF),
            pltpu.VMEM((2, far_rows, width), HALF),
            pltpu.VMEM((2, near_rows, width), HALF),
            pltpu.VMEM((2 * R * far_rows + 8, LANES), FULL),
            pltpu.VMEM((2 * (R + 1) * near_rows + 8, LANES), FULL),
            pltpu.VMEM((2 * max(sum(strides), piece), LANES), FULL),
            pltpu.VMEM((first_blocks, piece, width), FULL),
            pltpu.VMEM((2, counts[1], LANES), FULL),
            pltpu.VMEM((counts[2], (R + 1) * width), HALF),
            pltpu.VMEM((counts[2], LANES), FULL),
            pltpu.VMEM((first_blocks, piece, width), HALF),
            pltpu.VMEM((first_blocks, piece, width), HALF),
            pltpu.VMEM((counts[2], width), FULL),
            pltpu.VMEM((1, LANES), FULL),
            pltpu.VMEM((devices, 1, LANES), FULL),
            pltpu.SemaphoreType.DMA((LOADS,)),
            pltpu.SemaphoreType.DMA((2,)),
            pltpu.SemaphoreType.DMA((5,)),
            pltpu.SemaphoreType.DMA(()),
            pltpu.SemaphoreType.DMA(()),
        ]
        + [pltpu.SemaphoreType.DMA((2,))] * 6
        + [pltpu.SemaphoreType.DMA(())] * 4,
        compiler_params=pltpu.CompilerParams(
            collective_id=0, has_side_effects=True, vmem_limit_bytes=67043328
        ),
        name="fetch",
    )(*owners, *rows, *kinds, features, w_first, w_second, mask)


def shards(
    features,
    w_first,
    w_second,
    seed_owner,
    seed_row,
    hop1_owner,
    hop1_row,
    hop1_rel,
    hop2_owner,
    hop2_row,
    hop2_rel,
    edge_mask,
):
    devices = lax.axis_size("dom")
    counts = (hop2_row.shape[0], hop1_row.shape[0], seed_row.shape[0])
    caps = tuple((2 * length + devices - 1) // devices for length in counts)

    owners = [owner.reshape(1, -1) for owner in (hop2_owner, hop1_owner, seed_owner)]
    rows = [hop2_row.reshape(-1, LANES), hop1_row.reshape(-1, LANES), seed_row.reshape(1, -1)]
    edge_loss, mean_loss = fetch(
        owners,
        rows,
        [rel.reshape(-1, LANES) for rel in (hop2_rel, hop1_rel)],
        features,
        w_first,
        w_second,
        edge_mask.reshape(-1, BLOCK),
        caps,
        counts,
        devices,
    )
    return (edge_loss.reshape(-1), mean_loss[0, 0])


def solution(mesh):
    placed = (
        P("dom", None),
        P(),
        P(),
        P("dom", None),
        P("dom"),
        P("dom", None),
        P("dom"),
        P("dom"),
        P("dom", None),
        P("dom"),
        P("dom"),
        P("dom"),
    )
    return jax.shard_map(
        shards, mesh=mesh, in_specs=placed, out_specs=(P("dom"), P()), check_vma=False
    )
```

time: 113 us -> 94 us (0.83)
  Pallas kernels: 106 us -> 89 us
  local copies, waits for them, and re-layouts: 5.19 us -> 2.41 us
    pallas_call x1, Pallas kernels: 106 us -> 89 us  [fetch(): pl.pallas_call(functools.partial(fetch_kernel, devices, caps, strides, co...]
    reshape x2 -> x1, local copies, waits for them, and re-layouts: 2.75 us -> 1.27 us  [shards(): seed_row.reshape(1, -1)]
    pad x1 -> x0, local copies, waits for them, and re-layouts: 1.26 us -> none  [flat(): jnp.pad(values, ((0, 0), (0, spare)), constant_values=filler)]
where the time goes in v2:
time: 94 us; the launch traced here: 93.8 us
  Pallas kernels  89 us (95%)
  local copies, waits for them, and re-layouts  2.41 us (3%)
  between operations  2.4 us (3%)
    pallas_call x1, Pallas kernels, fetch(): pl.pallas_call(functools.partial(fetch_kernel, devices, caps, strides, co...  89 us

profile of v2, /device:TPU:0, one launch (start us, length us, event | category | flops | bytes accessed | tf_op | source)
XLA Modules:
  0.0 93.8 jit_solution(9036500120124359235)
XLA Ops:
  0.6 1.3 %reshape.39.seed_row = s32[1,288]{1,0:T(1,128)} reshape(s32[288]{0:T(512)} %param.16) | data formatting | bytes 2304 | tf_op jit(solution)/shard_map/reshape | solution.py:679
  1.9 89.0 %fetch.1 = (f32[1,128]{1,0:T(1,128)}, f32[1,1]{1,0:T(1,128)}) custom-call(s32[1,2304]{1,0:T(1,128)} %bitcast.12, s32[1,1152]{1,0:T(1,128)} %bitcast.15, s32[1,288]{1,0:T(1,128)} %bitcast.16, s32[18,128]{1,0:T(8,128)} %bitcast.10, s32[9,128]{1,0:T(8,128)} %bitcast.13, s32[1,288]{1,0:T(1,128)} %reshape.39.seed_row, s32[18,128]{1,0:T(8,128)} %bitcast.11, ...), custom_call_target="tpu_custom_call" | custom-call | tf_op jit(solution)/shard_map/fetch/pallas_call | solution.py:603
  90.9 1.1 %copy.16 = f32[128]{0:T(128)} copy(f32[128]{0:T(128)} %bitcast.18) | data formatting | bytes 1024

commit v3 on v2

--- a/solution.py
+++ b/solution.py
@@ -9,7 +9,6 @@
 
 MESH = pl.DeviceIdType.MESH
 HOP = 11
-ROWS = 96
 LANES = 128
 LOADS = 8
 SLOTS = 4
@@ -145,7 +144,6 @@
     staging,
     mine,
     hop_layer,
-    seed_input,
     kind_columns,
     piece_send,
     piece_recv,
@@ -202,7 +200,7 @@
     spare_owner[...] = jnp.full(spare_owner.shape, -1, jnp.int32)
     spare_row[...] = jnp.zeros(spare_row.shape, jnp.int32)
     spare_owner[0:1, 0:seed_count] = seed_owner[...]
-    spare_row[0:1, 0:seed_count] = seed_row[...]
+    spare_row[0:1, 0:seed_count] = seed_row[...].reshape(1, seed_count)
     far_blocks, first_blocks = far_row.shape[0], first_row.shape[0]
     seed_blocks = spare_row.shape[1] // LANES
     lanes_of = [slice(block * LANES, (block + 1) * LANES) for block in range(far_blocks)]
@@ -336,9 +334,15 @@
     others = pl.ds(0, devices - 1)
     pltpu.make_async_copy(requests.at[others], arrived.at[others], ask_send).wait()
     pltpu.make_async_copy(requests.at[others], arrived.at[others], ask_recv).wait()
-    move = pltpu.make_async_copy(arrived, wanted, small_sem.at[0])
-    move.start()
-    move.wait()
+    moves = []
+    for turn in range(2):
+        clients = pl.ds(lax.rem(half + turn, 2) * side, side)
+        moves.append(
+            pltpu.make_async_copy(arrived.at[clients], wanted.at[clients], small_sem.at[5 + turn])
+        )
+    moves[1].start()
+    moves[0].start()
+    moves[1].wait()
 
     def serve(turn):
         whose = lax.rem(half + turn, 2) * side
@@ -377,6 +381,7 @@
         lax.fori_loop(1, side + 1, one, 0)
 
     serve(1)
+    moves[0].wait()
     serve(0)
 
     far_cast[2 * far_zero : 2 * far_zero + 8, :] = jnp.zeros((8, LANES), FULL)
@@ -470,7 +475,7 @@
             src_ref=piece_send.at[block],
             dst_ref=piece_recv.at[block],
             send_sem=piece_send_sem,
-            recv_sem=piece_recv_sem,
+            recv_sem=piece_recv_sem.at[block],
             device_id=(mirror,),
             device_id_type=MESH,
         ).start()
@@ -490,44 +495,36 @@
 
     lax.fori_loop(0, first_blocks, own_block, 0)
 
-    pltpu.make_async_copy(piece_recv, piece_recv, piece_recv_sem).wait()
-
     def join(block, carry):
+        pltpu.make_async_copy(
+            piece_recv.at[block], piece_recv.at[block], piece_recv_sem.at[block]
+        ).wait()
         value = jnp.maximum(mine[block] + piece_recv[block].astype(FULL), 0.0).astype(HALF)
-        hops = pl.ds(pl.multiple_of(block * LANES, LANES), LANES)
         for part_of in range(2):
-            hop_layer[part_of, hops, :] = value[:LANES, lanes_of[part_of]].astype(FULL)
-        seeds = pl.ds(pl.multiple_of(block * seed_lanes, seed_lanes), seed_lanes)
-        seed_input[seeds, 0:width] = value[LANES:]
-        return carry
-
-    lax.fori_loop(0, first_blocks, join, 0)
-
-    def means(turn, carry):
-        start = pl.multiple_of(turn * ROWS, ROWS)
-        where = pl.ds(start, ROWS)
+            hop_layer[part_of] = value[:LANES, lanes_of[part_of]].astype(FULL)
         values = [
             jnp.concatenate(
-                [
-                    hop_layer[part_of, pl.ds(start * FAN1 + k, ROWS, stride=FAN1), :]
-                    for part_of in range(2)
-                ],
+                [hop_layer[part_of, pl.ds(k, seed_lanes, stride=FAN1), :] for part_of in range(2)],
                 axis=1,
             )
             for k in range(FAN1)
         ]
-        columns = kind_columns[where, :]
+        seeds = pl.ds(pl.multiple_of(block * seed_lanes, seed_lanes), seed_lanes)
+        columns = kind_columns[seeds, :]
+        inputs = [value[LANES:]]
         for kind in range(R):
             hot = [columns[:, k * R + kind : k * R + kind + 1] for k in range(FAN1)]
             portion = 1.0 / jnp.maximum(sum(hot[1:], hot[0]), 1.0)
             mean = (hot[0] * portion) * values[0]
             for k in range(1, FAN1):
                 mean = mean + (hot[k] * portion) * values[k]
-            seed_input[where, (kind + 1) * width : (kind + 2) * width] = mean.astype(HALF)
+            inputs.append(mean.astype(HALF))
+        second[seeds, :] = jnp.dot(
+            jnp.concatenate(inputs, axis=1), second_weights[...], preferred_element_type=FULL
+        )
         return carry
 
-    lax.fori_loop(0, seed_count // ROWS, means, 0)
-    second[...] = jnp.dot(seed_input[...], second_weights[...], preferred_element_type=FULL)
+    lax.fori_loop(0, first_blocks, join, 0)
 
     blocks = mask.shape[0]
     positives = blocks * BLOCK
@@ -634,8 +631,7 @@
             pltpu.VMEM((2 * (R + 1) * near_rows + 8, LANES), FULL),
             pltpu.VMEM((2 * max(sum(strides), piece), LANES), FULL),
             pltpu.VMEM((first_blocks, piece, width), FULL),
-            pltpu.VMEM((2, counts[1], LANES), FULL),
-            pltpu.VMEM((counts[2], (R + 1) * width), HALF),
+            pltpu.VMEM((2, LANES, LANES), FULL),
             pltpu.VMEM((counts[2], LANES), FULL),
             pltpu.VMEM((first_blocks, piece, width), HALF),
             pltpu.VMEM((first_blocks, piece, width), HALF),
@@ -644,12 +640,14 @@
             pltpu.VMEM((devices, 1, LANES), FULL),
             pltpu.SemaphoreType.DMA((LOADS,)),
             pltpu.SemaphoreType.DMA((2,)),
-            pltpu.SemaphoreType.DMA((5,)),
+            pltpu.SemaphoreType.DMA((7,)),
             pltpu.SemaphoreType.DMA(()),
             pltpu.SemaphoreType.DMA(()),
         ]
         + [pltpu.SemaphoreType.DMA((2,))] * 6
-        + [pltpu.SemaphoreType.DMA(())] * 4,
+        + [pltpu.SemaphoreType.DMA(())]
+        + [pltpu.SemaphoreType.DMA((first_blocks,))]
+        + [pltpu.SemaphoreType.DMA(())] * 2,
         compiler_params=pltpu.CompilerParams(
             collective_id=0, has_side_effects=True, vmem_limit_bytes=67043328
         ),
@@ -676,7 +674,7 @@
     caps = tuple((2 * length + devices - 1) // devices for length in counts)
 
     owners = [owner.reshape(1, -1) for owner in (hop2_owner, hop1_owner, seed_owner)]
-    rows = [hop2_row.reshape(-1, LANES), hop1_row.reshape(-1, LANES), seed_row.reshape(1, -1)]
+    rows = [hop2_row.reshape(-1, LANES), hop1_row.reshape(-1, LANES), seed_row]
     edge_loss, mean_loss = fetch(
         owners,
         rows,

time: 94 us -> 94.2 us (level)
  Pallas kernels: 89 us -> 90.4 us
  local copies, waits for them, and re-layouts: 2.41 us -> 1.11 us
    pallas_call x1, Pallas kernels: 89 us -> 90.4 us  [fetch(): pl.pallas_call(functools.partial(fetch_kernel, devices, caps, strides, co...]
    reshape x1 -> x0, local copies, waits for them, and re-layouts: 1.27 us -> none  [shards(): seed_row.reshape(1, -1)]
where the time goes in v3:
time: 94.2 us; the launch traced here: 94 us
  Pallas kernels  90.4 us (96%)
  between operations  2.41 us (3%)
  local copies, waits for them, and re-layouts  1.11 us (1%)
    pallas_call x1, Pallas kernels, fetch(): pl.pallas_call(functools.partial(fetch_kernel, devices, caps, strides, co...  90.4 us

profile of v3, /device:TPU:0, one launch (start us, length us, event | category | flops | bytes accessed | tf_op | source)
XLA Modules:
  0.0 94.0 jit_solution(8428836336501819111)
XLA Ops:
  0.6 90.4 %fetch.1 = (f32[1,128]{1,0:T(1,128)}, f32[1,1]{1,0:T(1,128)}) custom-call(s32[1,2304]{1,0:T(1,128)} %bitcast.12, s32[1,1152]{1,0:T(1,128)} %bitcast.15, s32[1,288]{1,0:T(1,128)} %bitcast.16, s32[18,128]{1,0:T(8,128)} %bitcast.10, s32[9,128]{1,0:T(8,128)} %bitcast.13, s32[288]{0:T(512)} %seed_row.1, s32[18,128]{1,0:T(8,128)} %bitcast.11, s32[9,128]{1,0:T(8,128)} %bitcast.14, ...), custom_call_target="tpu_custom_call" | custom-call | tf_op jit(solution)/shard_map/fetch/pallas_call | solution.py:600
  91.1 1.1 %copy.16 = f32[128]{0:T(128)} copy(f32[128]{0:T(128)} %bitcast.18) | data formatting | bytes 1024

commit v4 on v3

--- a/solution.py
+++ b/solution.py
@@ -142,6 +142,7 @@
     far_cast,
     near_cast,
     staging,
+    far_total,
     mine,
     hop_layer,
     kind_columns,
@@ -344,45 +345,42 @@
     moves[0].start()
     moves[1].wait()
 
-    def serve(turn):
+    def serve(turn, first, stride, send, recv, send_sem, recv_sem):
         whose = lax.rem(half + turn, 2) * side
-        parts = (
-            (0, far_stride, far_send, far_recv, far_send_sem, far_recv_sem),
-            (far_stride, near_stride, near_send, near_recv, near_send_sem, near_recv_sem),
-        )
 
         def one(step, carry):
             relay = lax.rem(local + step * HOP, side)
             client = whose + relay
-            for first, stride, send, recv, send_sem, recv_sem in parts:
-                for place in range(first, first + stride):
-                    row = table[pl.ds(wanted[client, 0, place], 2), :]
-                    staging[2 * place : 2 * place + 2, :] = row
-                send[client] = paired(staging, 2 * first, stride).astype(HALF)
-                where = pl.ds(pl.multiple_of(local * stride, stride), stride)
-
-                @pl.when(step < side)
-                def _():
-                    pltpu.make_async_remote_copy(
-                        src_ref=send.at[client],
-                        dst_ref=recv.at[turn, where],
-                        send_sem=send_sem.at[turn],
-                        recv_sem=recv_sem.at[turn],
-                        device_id=(half * side + relay,),
-                        device_id_type=MESH,
-                    ).start()
-
-                @pl.when(step == side)
-                def _():
-                    recv[turn, where, :] = send[client]
+            for place in range(stride):
+                row = table[pl.ds(wanted[client, 0, first + place], 2), :]
+                staging[2 * place : 2 * place + 2, :] = row
+            send[client] = paired(staging, 0, stride).astype(HALF)
+            where = pl.ds(pl.multiple_of(local * stride, stride), stride)
+
+            @pl.when(step < side)
+            def _():
+                pltpu.make_async_remote_copy(
+                    src_ref=send.at[client],
+                    dst_ref=recv.at[turn, where],
+                    send_sem=send_sem.at[turn],
+                    recv_sem=recv_sem.at[turn],
+                    device_id=(half * side + relay,),
+                    device_id_type=MESH,
+                ).start()
+
+            @pl.when(step == side)
+            def _():
+                recv[turn, where, :] = send[client]
 
             return carry
 
         lax.fori_loop(1, side + 1, one, 0)
 
-    serve(1)
-    moves[0].wait()
-    serve(0)
+    for turn in (1, 0):
+        if turn == 0:
+            moves[0].wait()
+        serve(turn, 0, far_stride, far_send, far_recv, far_send_sem, far_recv_sem)
+        serve(turn, far_stride, near_stride, near_send, near_recv, near_send_sem, near_recv_sem)
 
     far_cast[2 * far_zero : 2 * far_zero + 8, :] = jnp.zeros((8, LANES), FULL)
     near_cast[2 * near_zero : 2 * near_zero + 8, :] = jnp.zeros((8, LANES), FULL)
@@ -438,39 +436,48 @@
 
         lax.fori_loop(0, 2, some, 0)
 
-    def sums(turn, block, target):
-        look_row, share_row = turn * looks, turn * shared
-
-        def at(cast, row, lane_of):
-            return cast[pl.ds(look[look_row + row, 0, lane_of], 2), :]
-
+    def at(cast, turn, row, lane_of):
+        return cast[pl.ds(look[turn * looks + row, 0, lane_of], 2), :]
+
+    def far_sums(turn):
+        def one(block, carry):
+            for item in range(LANES):
+                row, first = (item * FAN2) // LANES, (item * FAN2) % LANES
+                total = at(far_cast, turn, block * FAN2 + row, first)
+                for k in range(1, FAN2):
+                    total = total + at(far_cast, turn, block * FAN2 + row, first + k)
+                scale = share[turn * shared + block * FAN2 + row, 0, first]
+                far_total[block, 2 * item : 2 * item + 2, :] = scale * total
+            return carry
+
+        lax.fori_loop(0, first_blocks, one, 0)
+
+    def sums(turn, block):
         for item in range(LANES):
-            row, first = (item * FAN2) // LANES, (item * FAN2) % LANES
-            total = at(far_cast, block * FAN2 + row, first)
-            for k in range(1, FAN2):
-                total = total + at(far_cast, block * FAN2 + row, first + k)
-            scale = share[share_row + block * FAN2 + row, 0, first]
-            target[2 * item : 2 * item + 2, :] = (
-                at(near_cast, first_base + block, item) + scale * total
+            place = 2 * item
+            staging[place : place + 2, :] = (
+                at(near_cast, turn, first_base + block, item)
+                + far_total[block, place : place + 2, :]
             )
         for seed in range(seed_lanes):
-            total = at(near_cast, seed_base + block, seed)
+            total = at(near_cast, turn, seed_base + block, seed)
             for k in range(FAN1):
                 item = seed * FAN1 + k
-                scale = share[share_row + far_blocks + block, 0, item]
-                total = total + scale * at(near_cast, turn_base + block, item)
+                scale = share[turn * shared + far_blocks + block, 0, item]
+                total = total + scale * at(near_cast, turn, turn_base + block, item)
             place = 2 * (LANES + seed)
-            target[place : place + 2, :] = total
+            staging[place : place + 2, :] = total
+        return paired(staging, 0, piece)
 
     piece = LANES + seed_lanes
     arrive(far_recv, 1, far_rows, far_stride, far_recv_sem)
     project(far_recv, 1, far_rows, far_cast, 1, R)
+    far_sums(1)
     arrive(near_recv, 1, near_rows, near_stride, near_recv_sem)
     project(near_recv, 1, near_rows, near_cast, 0, R + 1)
 
     def mirror_block(block, carry):
-        sums(1, block, staging)
-        piece_send[block] = paired(staging, 0, piece).astype(HALF)
+        piece_send[block] = sums(1, block).astype(HALF)
         pltpu.make_async_remote_copy(
             src_ref=piece_send.at[block],
             dst_ref=piece_recv.at[block],
@@ -485,12 +492,12 @@
 
     arrive(far_recv, 0, far_rows, far_stride, far_recv_sem)
     project(far_recv, 0, far_rows, far_cast, 1, R)
+    far_sums(0)
     arrive(near_recv, 0, near_rows, near_stride, near_recv_sem)
     project(near_recv, 0, near_rows, near_cast, 0, R + 1)
 
     def own_block(block, carry):
-        sums(0, block, staging)
-        mine[block] = paired(staging, 0, piece)
+        mine[block] = sums(0, block)
         return carry
 
     lax.fori_loop(0, first_blocks, own_block, 0)
@@ -630,6 +637,7 @@
             pltpu.VMEM((2 * R * far_rows + 8, LANES), FULL),
             pltpu.VMEM((2 * (R + 1) * near_rows + 8, LANES), FULL),
             pltpu.VMEM((2 * max(sum(strides), piece), LANES), FULL),
+            pltpu.VMEM((first_blocks, 2 * LANES, LANES), FULL),
             pltpu.VMEM((first_blocks, piece, width), FULL),
             pltpu.VMEM((2, LANES, LANES), FULL),
             pltpu.VMEM((counts[2], LANES), FULL),

time: 94.2 us -> 90.7 us (0.963)
  Pallas kernels: 90.4 us -> 87 us
    pallas_call x1, Pallas kernels: 90.4 us -> 87 us  [fetch(): pl.pallas_call(functools.partial(fetch_kernel, devices, caps, strides, co...]
where the time goes in v4:
time: 90.7 us; the launch traced here: 90.5 us
  Pallas kernels  87 us (96%)
  between operations  2.41 us (3%)
  local copies, waits for them, and re-layouts  1.11 us (1%)
    pallas_call x1, Pallas kernels, fetch(): pl.pallas_call(functools.partial(fetch_kernel, devices, caps, strides, co...  87 us

profile of v4, /device:TPU:0, one launch (start us, length us, event | category | flops | bytes accessed | tf_op | source)
XLA Modules:
  0.0 90.5 jit_solution(7830423641295406667)
XLA Ops:
  0.6 87.0 %fetch.1 = (f32[1,128]{1,0:T(1,128)}, f32[1,1]{1,0:T(1,128)}) custom-call(s32[1,2304]{1,0:T(1,128)} %bitcast.12, s32[1,1152]{1,0:T(1,128)} %bitcast.15, s32[1,288]{1,0:T(1,128)} %bitcast.16, s32[18,128]{1,0:T(8,128)} %bitcast.10, s32[9,128]{1,0:T(8,128)} %bitcast.13, s32[288]{0:T(512)} %seed_row.1, s32[18,128]{1,0:T(8,128)} %bitcast.11, s32[9,128]{1,0:T(8,128)} %bitcast.14, ...), custom_call_target="tpu_custom_call" | custom-call | tf_op jit(solution)/shard_map/fetch/pallas_call | solution.py:607
  87.6 1.1 %copy.16 = f32[128]{0:T(128)} copy(f32[128]{0:T(128)} %bitcast.18) | data formatting | bytes 1024

commit v5 on v4

--- a/solution.py
+++ b/solution.py
@@ -169,6 +169,7 @@
 ):
     me = lax.axis_index("dom")
     side = devices // 2
+    plane = side // 2
     half = lax.div(me, side)
     local = lax.rem(me, side)
     mirror = lax.rem(me + side, devices)
@@ -349,7 +350,9 @@
         whose = lax.rem(half + turn, 2) * side
 
         def one(step, carry):
-            relay = lax.rem(local + step * HOP, side)
+            across = lax.rem(step, 2)
+            its_plane = lax.rem(lax.div(local, plane) + across, 2)
+            relay = its_plane * plane + lax.rem(local + lax.div(step, 2), plane)
             client = whose + relay
             for place in range(stride):
                 row = table[pl.ds(wanted[client, 0, first + place], 2), :]
@@ -363,7 +366,7 @@
                     src_ref=send.at[client],
                     dst_ref=recv.at[turn, where],
                     send_sem=send_sem.at[turn],
-                    recv_sem=recv_sem.at[turn],
+                    recv_sem=recv_sem.at[turn, across],
                     device_id=(half * side + relay,),
                     device_id_type=MESH,
                 ).start()
@@ -415,15 +418,17 @@
     for keep in keeps:
         keep.wait()
 
-    def arrive(recv, turn, rows, stride, recv_sem):
-        there = pl.ds(0, rows - stride)
+    def arrive(recv, turn, across, stride, recv_sem):
+        there = pl.ds(0, (plane - 1 + across) * stride)
         block = recv.at[turn, there]
-        pltpu.make_async_copy(block, block, recv_sem.at[turn]).wait()
-
-    def project(recv, turn, rows, cast, first_kind_of, kinds):
+        pltpu.make_async_copy(block, block, recv_sem.at[turn, across]).wait()
+
+    def project(recv, turn, rows, cast, first_kind_of, kinds, stride, recv_sem):
         size = rows // 2
 
-        def some(part_of, carry):
+        for across in range(2):
+            arrive(recv, turn, across, stride, recv_sem)
+            part_of = lax.rem(lax.div(local, plane) + across, 2)
             start = pl.multiple_of(part_of * size, size)
             values = recv[turn, pl.ds(start, size), :]
             for kind in range(kinds):
@@ -432,9 +437,6 @@
                     values, first_weights[top : top + width, :], preferred_element_type=FULL
                 )
                 pair_up(cast, pl.multiple_of(2 * (kind * rows + start), 8), term)
-            return carry
-
-        lax.fori_loop(0, 2, some, 0)
 
     def at(cast, turn, row, lane_of):
         return cast[pl.ds(look[turn * looks + row, 0, lane_of], 2), :]
@@ -470,11 +472,9 @@
         return paired(staging, 0, piece)
 
     piece = LANES + seed_lanes
-    arrive(far_recv, 1, far_rows, far_stride, far_recv_sem)
-    project(far_recv, 1, far_rows, far_cast, 1, R)
+    project(far_recv, 1, far_rows, far_cast, 1, R, far_stride, far_recv_sem)
     far_sums(1)
-    arrive(near_recv, 1, near_rows, near_stride, near_recv_sem)
-    project(near_recv, 1, near_rows, near_cast, 0, R + 1)
+    project(near_recv, 1, near_rows, near_cast, 0, R + 1, near_stride, near_recv_sem)
 
     def mirror_block(block, carry):
         piece_send[block] = sums(1, block).astype(HALF)
@@ -490,11 +490,9 @@
 
     lax.fori_loop(0, first_blocks, mirror_block, 0)
 
-    arrive(far_recv, 0, far_rows, far_stride, far_recv_sem)
-    project(far_recv, 0, far_rows, far_cast, 1, R)
+    project(far_recv, 0, far_rows, far_cast, 1, R, far_stride, far_recv_sem)
     far_sums(0)
-    arrive(near_recv, 0, near_rows, near_stride, near_recv_sem)
-    project(near_recv, 0, near_rows, near_cast, 0, R + 1)
+    project(near_recv, 0, near_rows, near_cast, 0, R + 1, near_stride, near_recv_sem)
 
     def own_block(block, carry):
         mine[block] = sums(0, block)
@@ -652,7 +650,8 @@
             pltpu.SemaphoreType.DMA(()),
             pltpu.SemaphoreType.DMA(()),
         ]
-        + [pltpu.SemaphoreType.DMA((2,))] * 6
+        + [pltpu.SemaphoreType.DMA((2,))] * 2
+        + [pltpu.SemaphoreType.DMA((2,)), pltpu.SemaphoreType.DMA((2, 2))] * 2
         + [pltpu.SemaphoreType.DMA(())]
         + [pltpu.SemaphoreType.DMA((first_blocks,))]
         + [pltpu.SemaphoreType.DMA(())] * 2,

time: 90.7 us -> 89.8 us (0.990)
  Pallas kernels: 87 us -> 86 us
    pallas_call x1, Pallas kernels: 87 us -> 86 us  [fetch(): pl.pallas_call(functools.partial(fetch_kernel, devices, caps, strides, co...]
where the time goes in v5:
time: 89.8 us; the launch traced here: 89.5 us
  Pallas kernels  86 us (96%)
  between operations  2.41 us (3%)
  local copies, waits for them, and re-layouts  1.11 us (1%)
    pallas_call x1, Pallas kernels, fetch(): pl.pallas_call(functools.partial(fetch_kernel, devices, caps, strides, co...  86 us

profile of v5, /device:TPU:0, one launch (start us, length us, event | category | flops | bytes accessed | tf_op | source)
XLA Modules:
  0.0 89.5 jit_solution(14398628049743765986)
XLA Ops:
  0.6 86.0 %fetch.1 = (f32[1,128]{1,0:T(1,128)}, f32[1,1]{1,0:T(1,128)}) custom-call(s32[1,2304]{1,0:T(1,128)} %bitcast.12, s32[1,1152]{1,0:T(1,128)} %bitcast.15, s32[1,288]{1,0:T(1,128)} %bitcast.16, s32[18,128]{1,0:T(8,128)} %bitcast.10, s32[9,128]{1,0:T(8,128)} %bitcast.13, s32[288]{0:T(512)} %seed_row.1, s32[18,128]{1,0:T(8,128)} %bitcast.11, s32[9,128]{1,0:T(8,128)} %bitcast.14, ...), custom_call_target="tpu_custom_call" | custom-call | tf_op jit(solution)/shard_map/fetch/pallas_call | solution.py:605
  86.7 1.1 %copy.16 = f32[128]{0:T(128)} copy(f32[128]{0:T(128)} %bitcast.18) | data formatting | bytes 1024
